TPU v7x, 256 devices: a whole 4x4x8 slice. The times are simulated.
256 devices in a mesh: slab: 64 (over y, z, x_hi), load: 4 (over x_lo, core).
Axes of the slice: x: 4 (x_hi: 2, x_lo: 2; x = x_hi * 2 + x_lo), y: 4, z: 8, core: 2. Of those that a mesh axis runs over, the one named last changes fastest.
Arguments:
- start_disp: float32 [8, 3, 64, 64, 128], P('load', None, 'slab'), may hold values from -10 to 10
- density: float32 [64, 64, 128], P('slab'), may hold values from 0.05 to 1
- design: int32 [64, 64, 128], P('slab'), may hold values from 0 to 1, as said below
- support: int32 [64, 64, 128], P('slab'), may hold values 0 or 1
- load_nodes: int32 [8, 2048], P('load'), may hold values from 0 to 524287
- load_forces: float32 [8, 3, 2048], P('load'), may hold values from -6 to 6
Outputs:
- displacement: float32 [8, 3, 64, 64, 128], P('load', None, 'slab')
- new_density: float32 [64, 64, 128], P('slab')
Inputs may be any that keep to these rules, and one draw needn't show every extreme that they name: 1 marks an element of the design domain, 0 a void element; at least one element is in the design domain. `support`: 1 marks a node held fixed. `load_nodes`: flat node index z * 64 * 128 + x * 128 + y; a node may carry several forces of one load case.
All inputs are finite; a program needn't handle non-finite values. No bound on the sum of `support` on one device may be relied on, other than what follows from the above.
Results may differ from a plain program's by a relative error of at most 0.00024.
Values sent between devices are 32-bit elements; how exact they have to be, the bound alone decides.
A program may use at most 64 MiB of HBM per device.

v0:
```python
import jax
import jax.numpy as jnp
import numpy as np
from jax import lax
from jax.experimental import pallas as pl
from jax.experimental.pallas import tpu as pltpu
from jax.sharding import PartitionSpec as P

SWEEPS = 4
RADIUS = 2
POISSON = 0.3
STIFF_VOID = 0.001
UPPER_FACTOR = 1.2
LOWER_RATIO = 0.1
MOVE_LIMIT = 0.2
VOLUME_TARGET = 0.5
EPSILON = 1e-06
HIGHEST = lax.Precision.HIGHEST
MESH = pl.DeviceIdType.MESH
F32 = jnp.float32

NY_, NZ_ = 4, 8
LOADS_AX = 4
RING = 2 * LOADS_AX
PLANE = NY_ * NZ_
ROWS, COLS = 64, 128
POINTS = 2048
CHUNK = 256


def hex_stiffness():
    lame_first = POISSON / ((1 + POISSON) * (1 - 2 * POISSON))
    lame_shear = 1 / (2 * (1 + POISSON))
    elastic = np.zeros((6, 6))
    elastic[:3, :3] = lame_first
    for axis_a in range(3):
        elastic[axis_a, axis_a] += 2 * lame_shear
        elastic[3 + axis_a, 3 + axis_a] = lame_shear
    shear_pairs = ((0, 1), (1, 2), (0, 2))
    gauss_point = 1 / np.sqrt(3)
    matrix = np.zeros((24, 24))
    for quad_index in range(8):
        quad_coords = [
            gauss_point * (2 * (quad_index >> 2 - axis_a & 1) - 1) for axis_a in range(3)
        ]
        shape_grads = np.zeros((8, 3))
        for corner in range(8):
            corner_signs = [2 * (corner >> 2 - axis_a & 1) - 1 for axis_a in range(3)]
            for axis_a in range(3):
                deriv_value = float(corner_signs[axis_a])
                for axis_b in range(3):
                    if axis_b != axis_a:
                        deriv_value *= (1 + corner_signs[axis_b] * quad_coords[axis_b]) / 2
                shape_grads[corner, axis_a] = deriv_value
        strain = np.zeros((6, 24))
        for corner in range(8):
            for axis_a in range(3):
                strain[axis_a, 3 * corner + axis_a] = shape_grads[corner, axis_a]
            for pair_index, shear_pair in enumerate(shear_pairs):
                strain[3 + pair_index, 3 * corner + shear_pair[0]] = shape_grads[
                    corner, shear_pair[1]
                ]
                strain[3 + pair_index, 3 * corner + shear_pair[1]] = shape_grads[
                    corner, shear_pair[0]
                ]
        matrix += strain.T @ elastic @ strain / 8
    return matrix.astype(np.float32)


def mode_stiffness():
    ke = hex_stiffness().astype(np.float64)
    w = np.zeros((24, 24))
    for p in range(8):
        for o in range(8):
            sign = 1.0
            for a in range(3):
                if p >> (2 - a) & 1:
                    sign *= 1.0 if o >> (2 - a) & 1 else -1.0
            for c in range(3):
                w[3 * p + c, 3 * o + c] = sign
    return w @ ke @ w.T / 64


KHAT = mode_stiffness()
KD = float(hex_stiffness()[0, 0])


def kh(p, c, q, d):
    return float(KHAT[3 * p + c, 3 * q + d])


SHEAR = kh(1, 0, 1, 0)
TRACE = kh(1, 2, 2, 1)
NORMAL = kh(1, 2, 1, 2) - TRACE
TWIST = kh(3, 0, 5, 1)
BEND = kh(3, 1, 3, 1)
CROSS = kh(3, 1, 5, 0)
LAST = kh(7, 0, 7, 0)

SHEAR_PAIRS = (((1, 0), (4, 2)), ((1, 1), (2, 2)), ((2, 0), (4, 1)))
NORMALS = ((4, 0), (2, 1), (1, 2))
TWISTS = ((3, 0), (5, 1), (6, 2))
BENDS = (((3, 1), (5, 0)), ((3, 2), (6, 0)), ((5, 2), (6, 1)))


def check_table():
    table = np.zeros((24, 24))

    def put(a, b, v):
        table[3 * a[0] + a[1], 3 * b[0] + b[1]] = v

    for a, b in SHEAR_PAIRS:
        for u in (a, b):
            for v in (a, b):
                put(u, v, SHEAR)
    for a in NORMALS:
        for b in NORMALS:
            put(a, b, TRACE + (NORMAL if a == b else 0))
    for a in TWISTS:
        for b in TWISTS:
            put(a, b, 2 * TWIST if a == b else TWIST)
    for a, b in BENDS:
        put(a, a, BEND)
        put(b, b, BEND)
        put(a, b, CROSS)
        put(b, a, CROSS)
    for c in range(3):
        put((7, c), (7, c), LAST)
    assert np.abs(table - KHAT).max() < 1e-8


check_table()


def shift_rows_up(v, after, row):
    return pltpu.roll(jnp.where(row == 0, after, v), 7, 0)


def plane_modes(v, after, row, col):
    ahead = shift_rows_up(v, after, row)
    out = {}
    for px, f in ((0, v + ahead), (1, ahead - v)):
        fa = jnp.where(col == COLS - 1, 0.0, pltpu.roll(f, COLS - 1, 1))
        out[px, 0] = f + fa
        out[px, 1] = fa - f
    return out


def cell_modes(bottom, top):
    m = {}
    for c in range(3):
        for p in range(1, 8):
            xy = (p >> 1 & 1, p & 1)
            b, t = bottom[c][xy], top[c][xy]
            m[p, c] = t - b if p >> 2 else t + b
    return m


def cell_forces(m, stiff):
    f = {}
    shear, trace, normal = stiff * SHEAR, stiff * TRACE, stiff * NORMAL
    twist, bend, cross, last = stiff * TWIST, stiff * BEND, stiff * CROSS, stiff * LAST
    for a, b in SHEAR_PAIRS:
        f[a] = f[b] = shear * (m[a] + m[b])
    total = trace * (m[NORMALS[0]] + m[NORMALS[1]] + m[NORMALS[2]])
    for a in NORMALS:
        f[a] = total + normal * m[a]
    total = m[TWISTS[0]] + m[TWISTS[1]] + m[TWISTS[2]]
    for a in TWISTS:
        f[a] = twist * (total + m[a])
    for a, b in BENDS:
        f[a] = bend * m[a] + cross * m[b]
        f[b] = cross * m[a] + bend * m[b]
    for c in range(3):
        f[7, c] = last * m[7, c]
    return f


def cell_energy(m):
    shear = None
    for a, b in SHEAR_PAIRS:
        s = m[a] + m[b]
        shear = s * s if shear is None else shear + s * s
    total = m[NORMALS[0]] + m[NORMALS[1]] + m[NORMALS[2]]
    normal = m[NORMALS[0]] * m[NORMALS[0]] + m[NORMALS[1]] * m[NORMALS[1]] + m[NORMALS[2]] * m[NORMALS[2]]
    twist = m[TWISTS[0]] + m[TWISTS[1]] + m[TWISTS[2]]
    twists = twist * twist
    for a in TWISTS:
        twists = twists + m[a] * m[a]
    bends = None
    crosses = None
    for a, b in BENDS:
        s = m[a] * m[a] + m[b] * m[b]
        t = m[a] * m[b]
        bends = s if bends is None else bends + s
        crosses = t if crosses is None else crosses + t
    last = m[7, 0] * m[7, 0] + m[7, 1] * m[7, 1] + m[7, 2] * m[7, 2]
    return (
        SHEAR * shear
        + TRACE * (total * total)
        + NORMAL * normal
        + TWIST * twists
        + BEND * bends
        + (2.0 * CROSS) * crosses
        + LAST * last
    )


def gauss(count):
    t = (
        lax.broadcasted_iota(jnp.int32, (count, count), 0)
        - lax.broadcasted_iota(jnp.int32, (count, count), 1)
    ).astype(F32) * (1.0 / RADIUS)
    return jnp.exp(-(t * t))


def dot(a, b):
    return lax.dot_general(
        a, b, (((1,), (0,)), ((), ())), precision=HIGHEST, preferred_element_type=F32
    )


def total_of(tile):
    return jnp.sum(jnp.sum(tile, axis=0, keepdims=True), axis=1, keepdims=True)


def chebyshev(upper):
    lower = LOWER_RATIO * upper
    center = 0.5 * (upper + lower)
    half_width = 0.5 * (upper - lower)
    spread = center / half_width
    factor = 1.0 / spread
    zero = jnp.zeros_like(upper)
    e = [jnp.ones_like(upper)] + [zero] * (SWEEPS - 1)
    d = [1.0 / center] + [zero] * (SWEEPS - 1)
    u = [zero] * SWEEPS
    for sweep in range(SWEEPS):
        u = [a + b for a, b in zip(u, d)]
        if sweep < SWEEPS - 1:
            e = [e[0]] + [e[n] - d[n - 1] for n in range(1, SWEEPS)]
            after = 1.0 / (2.0 * spread - factor)
            d = [after * factor * a + 2.0 * after / half_width * b for a, b in zip(d, e)]
            factor = after
    return u


def kernel(
    u0_ref, dens_ref, des_ref, sup_ref, nodes_ref, forces_ref,
    disp_out, dens_out,
    t_buf, v_buf, u0_buf, rhs_buf, c_buf, sup_buf, stiff_buf, inv_buf, free_buf,
    tu_buf, send_buf, back_buf, coef_buf, dp_buf,
    fz_buf, ps_buf, fy_buf, smooth_buf, xq_buf, q_buf, num_buf, rs_buf, dt_buf, xt_buf,
    den_buf, sz_buf, sy_buf, wx_buf, wz_buf, wy_buf, vol_buf,
    recv, send, xsend, xrecv, zsend, zrecv, ysend, yrecv, vsend, vrecv,
):
    s = lax.axis_index("slab")
    l = lax.axis_index("load")
    h = lax.rem(s, 2)
    k = s // 2
    z = lax.rem(k, NZ_)
    y = k // NZ_
    j = h * LOADS_AX + l
    other = 1 - h

    def at(group, half=None, load=None):
        return {
            "slab": group * 2 + (h if half is None else half),
            "load": l if load is None else load,
        }

    above = lax.rem(k + 1, PLANE)
    below = lax.rem(k + PLANE - 1, PLANE)
    partner = at(k, half=other)

    def ring_peer(d):
        t = lax.rem(j + d, RING)
        return t, at(k, half=t // LOADS_AX, load=lax.rem(t, LOADS_AX))

    def z_peer(d):
        return at(y * NZ_ + lax.rem(z + d, NZ_))

    def y_peer(d):
        return at(lax.rem(y + d, NY_) * NZ_ + z)

    def plane_peer(dy, dz):
        return at(lax.rem(y + dy, NY_) * NZ_ + lax.rem(z + dz, NZ_))

    barrier = pltpu.get_barrier_semaphore()
    for d in range(1, RING):
        pl.semaphore_signal(barrier, inc=1, device_id=ring_peer(d)[1], device_id_type=MESH)
    for dy in range(NY_):
        for dz in range(NZ_):
            if dy or dz:
                pl.semaphore_signal(
                    barrier, inc=1, device_id=plane_peer(dy, dz), device_id_type=MESH
                )

    waits = []

    def remote(src, dst, ss, rs, device):
        copy = pltpu.make_async_remote_copy(
            src_ref=src, dst_ref=dst, send_sem=ss, recv_sem=rs,
            device_id=device, device_id_type=MESH,
        )
        copy.start()
        waits.append(copy)
        return copy

    row = lax.broadcasted_iota(jnp.int32, (8, COLS), 0)
    col = lax.broadcasted_iota(jnp.int32, (8, COLS), 1)

    dens = dens_ref[0]
    solid = des_ref[0].astype(F32) * dens
    c_buf[1 + h] = solid * solid * solid
    sup_buf[h] = sup_ref[0]
    free_own = 1.0 - sup_ref[0].astype(F32)
    for c in range(3):
        mine = u0_ref[h, c, 0]
        u0_buf[h, c] = mine
        t_buf[0, 1 + h, c, 0:ROWS] = mine * free_own
    zero8 = jnp.zeros((8, COLS), F32)
    for step in range(SWEEPS + 1):
        for n in range(4):
            for c in range(3):
                t_buf[step, n, c, ROWS : ROWS + 8] = zero8
    for n in range(1, 4):
        for c in range(3):
            tu_buf[n, c, ROWS : ROWS + 8] = zero8
    gauss_x, gauss_y = gauss(ROWS), gauss(COLS)
    smooth_buf[...] = dot(dot(gauss_x, dens), gauss_y)
    mine8 = pl.ds(pl.multiple_of(8 * j, 8), 8)
    jp = other * LOADS_AX + l
    other8 = pl.ds(pl.multiple_of(8 * jp, 8), 8)
    fz_buf[0, 0, h] = smooth_buf[mine8]
    dp_buf[h] = dens_ref[0, mine8]

    pl.semaphore_wait(barrier, RING - 1 + PLANE - 1)

    got_u0 = remote(u0_ref.at[other, :, 0], u0_buf.at[h], send.at[0], recv.at[0], partner)
    got_sup = remote(sup_ref.at[0], sup_buf.at[h], send.at[1], recv.at[1], partner)
    got_c = remote(c_buf.at[1 + h], c_buf.at[1 + h], send.at[2], recv.at[2], partner)
    toward = jnp.where(h == 0, below, above)
    away = jnp.where(h == 0, above, below)
    rows64 = pl.ds(0, ROWS)
    got_t1 = remote(
        t_buf.at[0, 1 + h, :, rows64], t_buf.at[0, 3 * other, :, rows64],
        send.at[3], recv.at[3], at(toward),
    )
    got_sm = remote(smooth_buf.at[other8], fz_buf.at[0, 0, h], send.at[4], recv.at[4], partner)
    got_dp = remote(dens_ref.at[0, other8], dp_buf.at[h], send.at[5], recv.at[5], partner)

    base = k * (2 * ROWS)
    wide = (2 * ROWS, CHUNK)
    line = lax.broadcasted_iota(jnp.int32, wide, 0)

    for n in range(2):
        for c in range(3):
            rhs_buf[n, c] = jnp.zeros((ROWS, COLS), F32)

    @pl.loop(0, POINTS // CHUNK)
    def _(i):
        cut = pl.ds(pl.multiple_of(i * CHUNK, CHUNK), CHUNK)
        node = jnp.where(h == 0, nodes_ref[0:1, cut], nodes_ref[1:2, cut])
        place = jnp.where((node >> 7) - base == line, 1.0, 0.0).astype(jnp.bfloat16)
        across = (node & 127) == line
        for c in range(3):
            force = jnp.where(h == 0, forces_ref[0, c : c + 1, cut], forces_ref[1, c : c + 1, cut])
            spread = jnp.where(across, force, 0.0)
            total = jnp.zeros((2 * ROWS, COLS), F32)
            for part in range(3):
                piece = spread.astype(jnp.bfloat16)
                total = total + lax.dot_general(
                    place, piece, (((1,), (1,)), ((), ())), preferred_element_type=F32
                )
                if part < 2:
                    spread = spread - piece.astype(F32)
            rhs_buf[0, c] += total[:ROWS]
            rhs_buf[1, c] += total[ROWS:]

    @pl.loop(0, NY_ * NZ_)
    def _(i):
        dy, dz = i // NZ_, lax.rem(i, NZ_)
        offset = 16 * (lax.rem(y + dy, NY_) - y) + 2 * (z - lax.rem(z + NZ_ - dz, NZ_))
        for a in range(3):
            t = jnp.full((8, COLS), offset + (a - 1), jnp.int32).astype(F32) * (1.0 / RADIUS)
            coef_buf[i * 3 + a] = jnp.exp(-(t * t))

    def z_send(which):
        return [
            remote(
                fz_buf.at[which, 0], fz_buf.at[which, d],
                zsend.at[which, d], zrecv.at[which, d], z_peer(d),
            )
            for d in range(1, NZ_)
        ]

    def z_mix(which, copies):
        for copy in copies:
            copy.wait_recv()

        @pl.loop(0, NY_)
        def _(dy):
            for a in range(2):
                total = None
                for d in range(NZ_):
                    for b in range(2):
                        term = coef_buf[dy * (3 * NZ_) + (3 * d + a - b + 1)] * fz_buf[which, d, b]
                        total = term if total is None else total + term
                ps_buf[which, dy, a] = total

        for a in range(2):
            fy_buf[which, 0, a] = ps_buf[which, 0, a]

    def y_send(which):
        return [
            remote(
                ps_buf.at[which, d], fy_buf.at[which, d],
                ysend.at[which, d], yrecv.at[which, d], y_peer(d),
            )
            for d in range(1, NY_)
        ]

    def y_sum(which, copies):
        for copy in copies:
            copy.wait_recv()
        return [
            fy_buf[which, 0, a] + fy_buf[which, 1, a] + fy_buf[which, 2, a] + fy_buf[which, 3, a]
            for a in range(2)
        ]

    got_c.wait_recv()
    got_up_c = remote(c_buf.at[2], c_buf.at[0], send.at[6], recv.at[6], at(above))
    got_sup.wait_recv()
    got_u0.wait_recv()
    free_other = 1.0 - sup_buf[other].astype(F32)
    for c in range(3):
        t_buf[0, 1 + other, c, 0:ROWS] = u0_buf[other, c] * free_other
    got_t2 = remote(
        t_buf.at[0, 1 + other, :, rows64], t_buf.at[0, 3 * h, :, rows64],
        send.at[7], recv.at[7], at(away),
    )
    for n in range(2):
        free_buf[n] = 1.0 - sup_buf[n].astype(F32)
    got_sm.wait_recv()
    got_dp.wait_recv()
    zs = z_send(0)

    has_below = jnp.where(k > 0, 1.0, 0.0)
    has_above = jnp.where(k < PLANE - 1, 1.0, 0.0)
    got_up_c.wait_recv()
    for e in range(3):
        stiff = STIFF_VOID + (1.0 - STIFF_VOID) * c_buf[e]
        stiff_buf[e] = stiff * has_below if e == 0 else stiff

    @pl.loop(0, ROWS // 8, init_carry=(zero8, zero8))
    def _(i, carry):
        rows = pl.ds(pl.multiple_of(i * 8, 8), 8)
        out = []
        for n in range(2):
            b = stiff_buf[n, rows] + stiff_buf[n + 1, rows]
            b = b + jnp.where(col == 0, 0.0, pltpu.roll(b, 1, 1))
            r = pltpu.roll(b, 1, 0)
            b = b + jnp.where(row == 0, carry[n], r)
            out.append(r)
            free = free_buf[n, rows]
            inv_buf[n, rows] = 1.0 / (free * KD * b + (1.0 - free))
        return tuple(out)

    def operate(step, finish, extra):
        def body(i, carry):
            behind, extra = list(carry[0]), carry[1]
            rows = pl.ds(pl.multiple_of(i * 8, 8), 8)
            after = pl.ds(pl.multiple_of(i * 8 + 8, 8), 8)
            total = [None, None]
            lower = None
            for n in range(4):
                upper = []
                for c in range(3):
                    v, w = t_buf[step, n, c, rows], t_buf[step, n, c, after]
                    if n == 3:
                        v, w = v * has_above, w * has_above
                    upper.append(plane_modes(v, w, row, col))
                if n:
                    e = n - 1
                    f = cell_forces(cell_modes(lower, upper), stiff_buf[e, rows])
                    for node, sign in ((e, 1.0), (e - 1, -1.0)):
                        if not 0 <= node < 2:
                            continue
                        part = {}
                        for c in range(3):
                            for q in range(4):
                                hi = f[4 + q, c]
                                if q == 0:
                                    value = hi if sign > 0 else -hi
                                else:
                                    value = f[q, c] + hi if sign > 0 else f[q, c] - hi
                                part[c, q] = value
                        if total[node] is None:
                            total[node] = part
                        else:
                            total[node] = {key: total[node][key] + part[key] for key in part}
                lower = upper
            for node in range(2):
                for c in range(3):
                    g = []
                    for px in range(2):
                        fs, fd = total[node][c, 2 * px], total[node][c, 2 * px + 1]
                        shifted = jnp.where(col == 0, 0.0, pltpu.roll(fs + fd, 1, 1))
                        g.append(fs - fd + shifted)
                    r = pltpu.roll(g[0] + g[1], 1, 0)
                    slot = 3 * node + c
                    value = g[0] - g[1] + jnp.where(row == 0, behind[slot], r)
                    behind[slot] = r
                    extra = finish(node, c, rows, value, extra)
            return tuple(behind), extra

        return lax.fori_loop(0, ROWS // 8, body, ((zero8,) * 6, extra))[1]

    def send_layers(step):
        up = remote(
            t_buf.at[step, 2, :, rows64], t_buf.at[step, 0, :, rows64],
            send.at[6 + 2 * step], recv.at[6 + 2 * step], at(above),
        )
        down = remote(
            t_buf.at[step, 1, :, rows64], t_buf.at[step, 3, :, rows64],
            send.at[7 + 2 * step], recv.at[7 + 2 * step], at(below),
        )
        return up, down

    def wait_layers(copies):
        for copy in copies:
            copy.wait_recv()

    def first(n, c, rows, value, extra):
        free, inv = free_buf[n, rows], inv_buf[n, rows]
        r = free * (rhs_buf[n, c, rows] - value) - (1.0 - free) * u0_buf[n, c, rows]
        g = r * inv
        v_buf[0, n, c, rows] = g
        t_buf[1, 1 + n, c, rows] = free * g
        return extra + r * g

    def later(step):
        def finish(n, c, rows, value, extra):
            free, inv = free_buf[n, rows], inv_buf[n, rows]
            v = v_buf[step - 1, n, c, rows]
            w = free * value + (1.0 - free) * v
            new = w * inv
            v_buf[step, n, c, rows] = new
            t_buf[step + 1, 1 + n, c, rows] = free * new
            return extra + v * w if step == 1 else extra

        return finish

    wait_layers((got_t1, got_t2))
    gr = operate(0, first, zero8)
    flight = send_layers(1)
    z_mix(0, zs)
    ys = y_send(0)
    wait_layers(flight)
    gw = operate(1, later(1), zero8)
    flight = send_layers(2)

    count8 = jnp.zeros((8, COLS), F32)
    for n in range(2):
        for i in range(ROWS // 8):
            count8 = count8 + jnp.where(c_buf[1 + n, 8 * i : 8 * i + 8] > 0.0, 1.0, 0.0)
    sums = [jnp.sum(t, axis=0, keepdims=True) for t in (gr, gw, count8)]
    tile = jnp.where(row == 0, sums[0], jnp.where(row == 1, sums[1], jnp.where(row == 2, sums[2], 0.0)))
    sz_buf[0] = tile
    scalar_z = [
        remote(sz_buf.at[0], sz_buf.at[d], zsend.at[3, d], zrecv.at[3, d], z_peer(d))
        for d in range(1, NZ_)
    ]
    denom = y_sum(0, ys)
    design_here = []
    for a in range(2):
        den_buf[a] = denom[a]
        fz_buf[1, 0, a] = jnp.where(c_buf[1 + a, mine8] > 0.0, 1.0, 0.0) / denom[a]
    zs = z_send(1)
    wait_layers(flight)
    operate(2, later(2), 0)
    flight = send_layers(3)
    for copy in scalar_z:
        copy.wait_recv()
    tile = sz_buf[0]
    for d in range(1, NZ_):
        tile = tile + sz_buf[d]
    sy_buf[0] = tile
    scalar_y = [
        remote(sy_buf.at[0], sy_buf.at[d], ysend.at[3, d], yrecv.at[3, d], y_peer(d))
        for d in range(1, NY_)
    ]
    z_mix(1, zs)
    ys = y_send(1)
    wait_layers(flight)
    operate(3, later(3), 0)
    got_last = remote(
        t_buf.at[4, 1, :, rows64], t_buf.at[4, 3, :, rows64],
        send.at[14], recv.at[14], at(below),
    )
    for copy in scalar_y:
        copy.wait_recv()
    tile = sy_buf[0] + sy_buf[1] + sy_buf[2] + sy_buf[3]
    gr_all = jnp.sum(tile[0:1], axis=1, keepdims=True)
    gw_all = jnp.sum(tile[1:2], axis=1, keepdims=True)
    count = jnp.sum(tile[2:3], axis=1, keepdims=True)
    coefs = [jnp.broadcast_to(c, (8, COLS)) for c in chebyshev(UPPER_FACTOR * gw_all / gr_all)]

    @pl.loop(0, ROWS // 8)
    def _(i):
        rows = pl.ds(pl.multiple_of(i * 8, 8), 8)
        for n in range(2):
            free = free_buf[n, rows]
            for c in range(3):
                u = u0_buf[n, c, rows]
                for power in range(SWEEPS):
                    u = u + coefs[power] * v_buf[power, n, c, rows]
                send_buf[n, c, rows] = u
                tu_buf[1 + n, c, rows] = free * u

    got_back = remote(send_buf.at[other], back_buf, send.at[15], recv.at[15], partner)
    for c in range(3):
        disp_out[h, c, 0] = send_buf[h, c]

    q8 = y_sum(1, ys)
    for a in range(2):
        xq_buf[0, a] = q8[a]

    def ring_send(which, src, dst):
        out = []
        for d in range(1, RING):
            t, device = ring_peer(d)
            out.append(remote(src(t), dst(d), xsend.at[which, d], xrecv.at[which, d], device))
        return out

    xs = ring_send(0, lambda t: xq_buf.at[0], lambda d: xq_buf.at[d])

    def energy(e):
        @pl.loop(0, ROWS // 8)
        def _(i):
            rows = pl.ds(pl.multiple_of(i * 8, 8), 8)
            after = pl.ds(pl.multiple_of(i * 8 + 8, 8), 8)
            planes = [
                [plane_modes(tu_buf[n, c, rows], tu_buf[n, c, after], row, col) for c in range(3)]
                for n in (e, e + 1)
            ]
            value = cell_energy(cell_modes(*planes))
            weight = (3.0 * (1.0 - STIFF_VOID)) * c_buf[e, rows]
            num_buf[e - 1, rows] = weight * value

    def smooth_xy(read):
        mixed = dot(jnp.concatenate([read(0), read(1)], 0), gauss_y)
        return [dot(gauss_x, mixed[ROWS * a : ROWS * a + ROWS]) for a in range(2)]

    energy(1)
    for copy in xs:
        copy.wait_recv()
    for d in range(RING):
        there = pl.ds(pl.multiple_of(8 * lax.rem(j + RING - d, RING), 8), 8)
        for a in range(2):
            q_buf[a, there] = xq_buf[d, a]
    q = smooth_xy(lambda a: q_buf[a])
    for a in range(2):
        q_buf[a] = q[a]

    got_last.wait_recv()

    @pl.loop(0, ROWS // 8)
    def _(i):
        rows = pl.ds(pl.multiple_of(i * 8, 8), 8)
        for c in range(3):
            u = t_buf[0, 3, c, rows]
            for power in range(SWEEPS):
                u = u + coefs[power] * t_buf[power + 1, 3, c, rows]
            tu_buf[3, c, rows] = u * has_above

    energy(2)
    part = jnp.zeros((8, COLS), F32)
    for a in range(2):
        for i in range(ROWS // 8):
            cut = slice(8 * i, 8 * i + 8)
            part = part + q_buf[a, cut] * num_buf[a, cut]
    wx_buf[0] = part
    wxs = ring_send(1, lambda t: wx_buf.at[0], lambda d: wx_buf.at[d])
    numer = smooth_xy(lambda a: num_buf[a])
    for a in range(2):
        num_buf[a] = numer[a]
    for a in range(2):
        rs_buf[0, a] = num_buf[a, mine8]
    xs = ring_send(
        2,
        lambda t: num_buf.at[:, pl.ds(pl.multiple_of(8 * t, 8), 8)],
        lambda d: rs_buf.at[d],
    )
    for copy in wxs:
        copy.wait_recv()
    tile = wx_buf[0]
    for d in range(1, RING):
        tile = tile + wx_buf[d]
    wz_buf[0] = tile
    wzs = [
        remote(wz_buf.at[0], wz_buf.at[d], zsend.at[4, d], zrecv.at[4, d], z_peer(d))
        for d in range(1, NZ_)
    ]
    for copy in xs:
        copy.wait_recv()
    for a in range(2):
        total = rs_buf[0, a]
        for d in range(1, RING):
            total = total + rs_buf[d, a]
        fz_buf[2, 0, a] = total
    zs = z_send(2)
    for copy in wzs:
        copy.wait_recv()
    tile = wz_buf[0]
    for d in range(1, NZ_):
        tile = tile + wz_buf[d]
    wy_buf[0] = tile
    wys = [
        remote(wy_buf.at[0], wy_buf.at[d], ysend.at[4, d], yrecv.at[4, d], y_peer(d))
        for d in range(1, NY_)
    ]
    z_mix(2, zs)
    ys = y_send(2)
    for copy in wys:
        copy.wait_recv()
    weighted_all = total_of(wy_buf[0] + wy_buf[1] + wy_buf[2] + wy_buf[3])
    inv_mean = 1.0 / (weighted_all / count + EPSILON)
    numer = y_sum(2, ys)
    for a in range(2):
        here = jnp.where(c_buf[1 + a, mine8] > 0.0, 1.0, 0.0)
        weighted = here * (numer[a] / den_buf[a])
        ratio = weighted * inv_mean
        old = dp_buf[a]
        trial = jnp.minimum(
            jnp.maximum(old * jnp.sqrt(ratio), old - MOVE_LIMIT), old + MOVE_LIMIT
        )
        xt_buf[0, a] = here * trial
    xs = ring_send(3, lambda t: xt_buf.at[0], lambda d: xt_buf.at[d])
    for copy in xs:
        copy.wait_recv()
    tile = None
    for d in range(RING):
        for a in range(2):
            tile = xt_buf[d, a] if tile is None else tile + xt_buf[d, a]
    vol_buf[0] = jnp.sum(tile, axis=0, keepdims=True)
    vs = [
        remote(
            vol_buf.at[0], vol_buf.at[dy * NZ_ + dz],
            vsend.at[dy * NZ_ + dz], vrecv.at[dy * NZ_ + dz], plane_peer(dy, dz),
        )
        for dy in range(NY_)
        for dz in range(NZ_)
        if dy or dz
    ]
    got_back.wait_recv()
    for c in range(3):
        disp_out[other, c, 0] = back_buf[c]
    for copy in vs:
        copy.wait_recv()
    tile = vol_buf[0]
    for i in range(1, PLANE):
        tile = tile + vol_buf[i]
    volume = jnp.sum(tile, axis=1, keepdims=True)
    scale = VOLUME_TARGET / (volume / count + EPSILON)
    for d in range(RING):
        there = pl.ds(pl.multiple_of(8 * lax.rem(j + RING - d, RING), 8), 8)
        dens_out[0, there] = jnp.minimum(scale * xt_buf[d, h], 1.0)
    for copy in waits:
        copy.wait_send()


def shards(start_disp, density, design, support, load_nodes, load_forces):
    vmem = lambda *shape: pltpu.VMEM(shape, F32)
    dma = lambda *shape: pltpu.SemaphoreType.DMA(shape)
    plane = (ROWS, COLS)
    return pl.pallas_call(
        kernel,
        out_shape=(
            jax.ShapeDtypeStruct(start_disp.shape, F32),
            jax.ShapeDtypeStruct(density.shape, F32),
        ),
        in_specs=[pl.BlockSpec(memory_space=pltpu.VMEM)] * 6,
        out_specs=(pl.BlockSpec(memory_space=pltpu.VMEM),) * 2,
        scratch_shapes=[
            vmem(SWEEPS + 1, 4, 3, ROWS + 8, COLS),
            vmem(SWEEPS, 2, 3, *plane),
            vmem(2, 3, *plane),
            vmem(2, 3, *plane),
            vmem(3, *plane),
            pltpu.VMEM((2, *plane), jnp.int32),
            vmem(3, *plane),
            vmem(2, *plane),
            vmem(2, *plane),
            vmem(4, 3, ROWS + 8, COLS),
            vmem(2, 3, *plane),
            vmem(3, *plane),
            vmem(3 * NY_ * NZ_, 8, COLS),
            vmem(2, 8, COLS),
            vmem(3, NZ_, 2, 8, COLS),
            vmem(3, NY_, 2, 8, COLS),
            vmem(3, NY_, 2, 8, COLS),
            vmem(*plane),
            vmem(RING, 2, 8, COLS),
            vmem(2, *plane),
            vmem(2, *plane),
            vmem(RING, 2, 8, COLS),
            vmem(2, 8, COLS),
            vmem(RING, 2, 8, COLS),
            vmem(2, 8, COLS),
            vmem(NZ_, 8, COLS),
            vmem(NY_, 8, COLS),
            vmem(RING, 8, COLS),
            vmem(NZ_, 8, COLS),
            vmem(NY_, 8, COLS),
            vmem(PLANE, 1, COLS),
            dma(16), dma(16),
            dma(4, RING), dma(4, RING),
            dma(5, NZ_), dma(5, NZ_),
            dma(5, NY_), dma(5, NY_),
            dma(PLANE), dma(PLANE),
        ],
        compiler_params=pltpu.CompilerParams(
            collective_id=0, has_side_effects=True, vmem_limit_bytes=48 * 1024 * 1024
        ),
    )(start_disp, density, design, support, load_nodes, load_forces)


def solution(mesh):
    return jax.shard_map(
        shards,
        mesh=mesh,
        in_specs=(
            P("load", None, "slab", None, None),
            P("slab", None, None),
            P("slab", None, None),
            P("slab", None, None),
            P("load", None),
            P("load", None, None),
        ),
        out_specs=(P("load", None, "slab", None, None), P("slab", None, None)),
        check_vma=False,
    )
```

profile of v0, /device:TPU:1, one launch (start us, length us, event | category | flops | bytes accessed | tf_op | source)
XLA Modules:
  0.0 79.9 jit_solution(8704161001095460410)
XLA Ops:
  0.6 0.0 copy-start.4
  0.6 0.0 copy-start.3
  0.7 0.0 copy-start.2
  0.7 0.0 copy-start.1
  0.7 0.9 %copy.8.forces_ref = f32[2,3,2048]{2,1,0:T(4,128)S(1)} copy(f32[2,3,2048]{2,0,1:T(2,128)} %param.11) | data formatting | bytes 98304 | tf_op args[5]
  1.5 0.0 copy-done.4
  1.5 0.0 copy-done.3
  1.6 0.0 copy-done.2
  1.6 0.0 copy-done.1
  1.6 0.0 copy-start
  1.6 0.9 %copy-done = f32[2,3,1,64,128]{4,3,2,1,0:T(8,128)S(1)} copy-done((f32[2,3,1,64,128]{4,3,2,1,0:T(8,128)S(1)}, f32[2,3,1,64,128]{4,3,2,1,0:T(8,128)}, u32[]{:S(2)}) %copy-start) | copy-done | bytes 196632
  2.5 76.1 %shard_map.77 = (f32[2,3,1,64,128]{4,3,2,1,0:T(8,128)S(1)}, f32[1,64,128]{2,1,0:T(8,128)S(1)}) custom-call(f32[2,3,1,64,128]{4,3,2,1,0:T(8,128)S(1)} %copy-done, f32[1,64,128]{2,1,0:T(8,128)S(1)} %copy-done.1, s32[1,64,128]{2,1,0:T(8,128)S(1)} %copy-done.2, s32[1,64,128]{2,1,0:T(8,128)S(1)} %copy-done.3, s32[2,2048]{1,0:T(2,128)S(1)} %copy-done.4, ...), custom_call_target="tpu_custom_call" | custom-call | tf_op jit(solution)/shard_map/pallas_call | solution.py:777
  78.6 0.7 copy.11
  79.3 0.6 copy.12
Async XLA Ops:
  0.6 0.9 %copy-start.4 = (s32[2,2048]{1,0:T(2,128)S(1)}, s32[2,2048]{1,0:T(2,128)}, u32[]{:S(2)}) copy-start(s32[2,2048]{1,0:T(2,128)} %nodes_ref.1) | copy-start | bytes 49156
  0.6 0.9 %copy-start.3 = (s32[1,64,128]{2,1,0:T(8,128)S(1)}, s32[1,64,128]{2,1,0:T(8,128)}, u32[]{:S(2)}) copy-start(s32[1,64,128]{2,1,0:T(8,128)} %sup_ref.1) | copy-start | bytes 98308
  0.7 0.9 %copy-start.2 = (s32[1,64,128]{2,1,0:T(8,128)S(1)}, s32[1,64,128]{2,1,0:T(8,128)}, u32[]{:S(2)}) copy-start(s32[1,64,128]{2,1,0:T(8,128)} %des_ref.1) | copy-start | bytes 98308
  0.7 0.9 %copy-start.1 = (f32[1,64,128]{2,1,0:T(8,128)S(1)}, f32[1,64,128]{2,1,0:T(8,128)}, u32[]{:S(2)}) copy-start(f32[1,64,128]{2,1,0:T(8,128)} %dens_ref.1) | copy-start | bytes 98308
  1.6 0.9 %copy-start = (f32[2,3,1,64,128]{4,3,2,1,0:T(8,128)S(1)}, f32[2,3,1,64,128]{4,3,2,1,0:T(8,128)}, u32[]{:S(2)}) copy-start(f32[2,3,1,64,128]{4,3,2,1,0:T(8,128)} %u0_ref.1) | copy-start | bytes 589828
where the time goes:
time: 80 us; the launch traced here: 79.9 us
  Pallas kernels  76.1 us (95%)
  local copies, waits for them, and re-layouts  3.09 us (4%)
    pallas_call x1, Pallas kernels, shards(): pl.pallas_call(kernel, out_shape=(jax.ShapeDtypeStruct(start_disp.shape,...  76.1 us
    unnamed x13, local copies, waits for them, and re-layouts  3.09 us

commit v1 on v0

v1 whole, which is shorter than its diff:
```python
import contextlib

import jax
import jax.numpy as jnp
import numpy as np
from jax import lax
from jax.experimental import pallas as pl
from jax.experimental.pallas import tpu as pltpu
from jax.sharding import PartitionSpec as P

SWEEPS = 4
RADIUS = 2
POISSON = 0.3
STIFF_VOID = 0.001
UPPER_FACTOR = 1.2
LOWER_RATIO = 0.1
MOVE_LIMIT = 0.2
VOLUME_TARGET = 0.5
EPSILON = 1e-06
HIGHEST = lax.Precision.HIGHEST
MESH = pl.DeviceIdType.MESH
F32 = jnp.float32

NY_, NZ_ = 4, 8
LOADS_AX = 4
RING = 2 * LOADS_AX
PLANE = NY_ * NZ_
ROWS, COLS = 64, 128
POINTS = 2048
CHUNK = 256
PIECE = 16
PIECES = ROWS // PIECE


def hex_stiffness():
    lame_first = POISSON / ((1 + POISSON) * (1 - 2 * POISSON))
    lame_shear = 1 / (2 * (1 + POISSON))
    elastic = np.zeros((6, 6))
    elastic[:3, :3] = lame_first
    for axis_a in range(3):
        elastic[axis_a, axis_a] += 2 * lame_shear
        elastic[3 + axis_a, 3 + axis_a] = lame_shear
    shear_pairs = ((0, 1), (1, 2), (0, 2))
    gauss_point = 1 / np.sqrt(3)
    matrix = np.zeros((24, 24))
    for quad_index in range(8):
        quad_coords = [
            gauss_point * (2 * (quad_index >> 2 - axis_a & 1) - 1) for axis_a in range(3)
        ]
        shape_grads = np.zeros((8, 3))
        for corner in range(8):
            corner_signs = [2 * (corner >> 2 - axis_a & 1) - 1 for axis_a in range(3)]
            for axis_a in range(3):
                deriv_value = float(corner_signs[axis_a])
                for axis_b in range(3):
                    if axis_b != axis_a:
                        deriv_value *= (1 + corner_signs[axis_b] * quad_coords[axis_b]) / 2
                shape_grads[corner, axis_a] = deriv_value
        strain = np.zeros((6, 24))
        for corner in range(8):
            for axis_a in range(3):
                strain[axis_a, 3 * corner + axis_a] = shape_grads[corner, axis_a]
            for pair_index, shear_pair in enumerate(shear_pairs):
                strain[3 + pair_index, 3 * corner + shear_pair[0]] = shape_grads[
                    corner, shear_pair[1]
                ]
                strain[3 + pair_index, 3 * corner + shear_pair[1]] = shape_grads[
                    corner, shear_pair[0]
                ]
        matrix += strain.T @ elastic @ strain / 8
    return matrix.astype(np.float32)


def mode_stiffness():
    ke = hex_stiffness().astype(np.float64)
    w = np.zeros((24, 24))
    for p in range(8):
        for o in range(8):
            sign = 1.0
            for a in range(3):
                if p >> (2 - a) & 1:
                    sign *= 1.0 if o >> (2 - a) & 1 else -1.0
            for c in range(3):
                w[3 * p + c, 3 * o + c] = sign
    return w @ ke @ w.T / 64


KHAT = mode_stiffness()
KD = float(hex_stiffness()[0, 0])


def kh(p, c, q, d):
    return float(KHAT[3 * p + c, 3 * q + d])


SHEAR = kh(1, 0, 1, 0)
TRACE = kh(1, 2, 2, 1)
NORMAL = kh(1, 2, 1, 2) - TRACE
TWIST = kh(3, 0, 5, 1)
BEND = kh(3, 1, 3, 1)
CROSS = kh(3, 1, 5, 0)
LAST = kh(7, 0, 7, 0)

SHEAR_PAIRS = (((1, 0), (4, 2)), ((1, 1), (2, 2)), ((2, 0), (4, 1)))
NORMALS = ((4, 0), (2, 1), (1, 2))
TWISTS = ((3, 0), (5, 1), (6, 2))
BENDS = (((3, 1), (5, 0)), ((3, 2), (6, 0)), ((5, 2), (6, 1)))


def check_table():
    table = np.zeros((24, 24))

    def put(a, b, v):
        table[3 * a[0] + a[1], 3 * b[0] + b[1]] = v

    for a, b in SHEAR_PAIRS:
        for u in (a, b):
            for v in (a, b):
                put(u, v, SHEAR)
    for a in NORMALS:
        for b in NORMALS:
            put(a, b, TRACE + (NORMAL if a == b else 0))
    for a in TWISTS:
        for b in TWISTS:
            put(a, b, 2 * TWIST if a == b else TWIST)
    for a, b in BENDS:
        put(a, a, BEND)
        put(b, b, BEND)
        put(a, b, CROSS)
        put(b, a, CROSS)
    for c in range(3):
        put((7, c), (7, c), LAST)
    assert np.abs(table - KHAT).max() < 1e-8


check_table()


def shift_rows_up(v, after, row):
    return pltpu.roll(jnp.where(row == 0, after, v), 7, 0)


def plane_modes(v, after, row, col):
    ahead = shift_rows_up(v, after, row)
    out = {}
    for px, f in ((0, v + ahead), (1, ahead - v)):
        fa = jnp.where(col == COLS - 1, 0.0, pltpu.roll(f, COLS - 1, 1))
        out[px, 0] = f + fa
        out[px, 1] = fa - f
    return out


def cell_modes(bottom, top):
    m = {}
    for c in range(3):
        for p in range(1, 8):
            xy = (p >> 1 & 1, p & 1)
            b, t = bottom[c][xy], top[c][xy]
            m[p, c] = t - b if p >> 2 else t + b
    return m


def cell_forces(m, stiff):
    f = {}
    shear, trace, normal = stiff * SHEAR, stiff * TRACE, stiff * NORMAL
    twist, bend, cross, last = stiff * TWIST, stiff * BEND, stiff * CROSS, stiff * LAST
    for a, b in SHEAR_PAIRS:
        f[a] = f[b] = shear * (m[a] + m[b])
    total = trace * (m[NORMALS[0]] + m[NORMALS[1]] + m[NORMALS[2]])
    for a in NORMALS:
        f[a] = total + normal * m[a]
    total = m[TWISTS[0]] + m[TWISTS[1]] + m[TWISTS[2]]
    for a in TWISTS:
        f[a] = twist * (total + m[a])
    for a, b in BENDS:
        f[a] = bend * m[a] + cross * m[b]
        f[b] = cross * m[a] + bend * m[b]
    for c in range(3):
        f[7, c] = last * m[7, c]
    return f


def cell_energy(m):
    shear = None
    for a, b in SHEAR_PAIRS:
        s = m[a] + m[b]
        shear = s * s if shear is None else shear + s * s
    total = m[NORMALS[0]] + m[NORMALS[1]] + m[NORMALS[2]]
    normal = m[NORMALS[0]] * m[NORMALS[0]] + m[NORMALS[1]] * m[NORMALS[1]] + m[NORMALS[2]] * m[NORMALS[2]]
    twist = m[TWISTS[0]] + m[TWISTS[1]] + m[TWISTS[2]]
    twists = twist * twist
    for a in TWISTS:
        twists = twists + m[a] * m[a]
    bends = None
    crosses = None
    for a, b in BENDS:
        s = m[a] * m[a] + m[b] * m[b]
        t = m[a] * m[b]
        bends = s if bends is None else bends + s
        crosses = t if crosses is None else crosses + t
    last = m[7, 0] * m[7, 0] + m[7, 1] * m[7, 1] + m[7, 2] * m[7, 2]
    return (
        SHEAR * shear
        + TRACE * (total * total)
        + NORMAL * normal
        + TWIST * twists
        + BEND * bends
        + (2.0 * CROSS) * crosses
        + LAST * last
    )


def gauss(count):
    t = (
        lax.broadcasted_iota(jnp.int32, (count, count), 0)
        - lax.broadcasted_iota(jnp.int32, (count, count), 1)
    ).astype(F32) * (1.0 / RADIUS)
    return jnp.exp(-(t * t))


def dot(a, b):
    return lax.dot_general(
        a, b, (((1,), (0,)), ((), ())), precision=HIGHEST, preferred_element_type=F32
    )


def total_of(tile):
    return jnp.sum(jnp.sum(tile, axis=0, keepdims=True), axis=1, keepdims=True)


def chebyshev(upper):
    lower = LOWER_RATIO * upper
    center = 0.5 * (upper + lower)
    half_width = 0.5 * (upper - lower)
    spread = center / half_width
    factor = 1.0 / spread
    zero = jnp.zeros_like(upper)
    e = [jnp.ones_like(upper)] + [zero] * (SWEEPS - 1)
    d = [1.0 / center] + [zero] * (SWEEPS - 1)
    u = [zero] * SWEEPS
    for sweep in range(SWEEPS):
        u = [a + b for a, b in zip(u, d)]
        if sweep < SWEEPS - 1:
            e = [e[0]] + [e[n] - d[n - 1] for n in range(1, SWEEPS)]
            after = 1.0 / (2.0 * spread - factor)
            d = [after * factor * a + 2.0 * after / half_width * b for a, b in zip(d, e)]
            factor = after
    return u


def kernel(
    u0_ref, dens_ref, des_ref, sup_ref, nodes_ref, forces_ref,
    disp_out, dens_out,
    t_buf, v_buf, u0_buf, rhs_buf, c_buf, stiff_buf, inv_buf, free_buf,
    swap_out, swap_in, tu_buf, send_buf, back_buf, coef_buf, row_out, row_in,
    fz_buf, ps_buf, fy_buf, smooth_buf, xq_buf, q_buf, num_buf, rs_buf, xt_buf,
    den_buf, sz_buf, sy_buf, wx_buf, wz_buf, wy_buf, vol_buf,
    swap_recv, halo_recv, c_recv, halo_send, one_send, one_recv, group_send, group_recv,
):
    s = lax.axis_index("slab")
    l = lax.axis_index("load")
    h = lax.rem(s, 2)
    k = s // 2
    z = lax.rem(k, NZ_)
    y = k // NZ_
    j = h * LOADS_AX + l
    other = 1 - h

    def at(group, half=None, load=None):
        return {
            "slab": group * 2 + (h if half is None else half),
            "load": l if load is None else load,
        }

    above = lax.rem(k + 1, PLANE)
    below = lax.rem(k + PLANE - 1, PLANE)
    partner = at(k, half=other)

    def ring_peer(d):
        t = lax.rem(j + d, RING)
        return t, at(k, half=t // LOADS_AX, load=lax.rem(t, LOADS_AX))

    def z_peer(d):
        return at(y * NZ_ + lax.rem(z + d, NZ_))

    def y_peer(d):
        return at(lax.rem(y + d, NY_) * NZ_ + z)

    def plane_peer(i):
        return at(lax.rem(y + i // NZ_, NY_) * NZ_ + lax.rem(z + i % NZ_, NZ_))

    phases = contextlib.ExitStack()

    def mark(name):
        phases.close()
        if name:
            phases.enter_context(jax.named_scope(name))

    mark("signals")
    barrier = pltpu.get_barrier_semaphore()
    for d in range(1, RING):
        pl.semaphore_signal(barrier, inc=1, device_id=ring_peer(d)[1], device_id_type=MESH)
    for i in range(1, PLANE):
        pl.semaphore_signal(barrier, inc=1, device_id=plane_peer(i), device_id_type=MESH)

    sent = []

    def start(src, dst, ss, rs, device):
        copy = pltpu.make_async_remote_copy(
            src_ref=src, dst_ref=dst, send_sem=ss, recv_sem=rs,
            device_id=device, device_id_type=MESH,
        )
        copy.start()
        return copy

    def whole(ref, ss, rs):
        return pltpu.make_async_remote_copy(
            src_ref=ref, dst_ref=ref, send_sem=ss, recv_sem=rs,
            device_id=partner, device_id_type=MESH,
        )

    def one(slot, src, dst, device):
        copy = start(src, dst, one_send.at[slot], one_recv.at[slot], device)
        sent.append(copy)
        return copy

    def group(slot, buf, count, src, peer):
        for d in range(1, count):
            start(src(d), buf.at[d], group_send.at[slot], group_recv.at[slot], peer(d))
        rest = whole(buf.at[pl.ds(1, count - 1)], group_send.at[slot], group_recv.at[slot])
        sent.append(rest)
        return rest

    row = lax.broadcasted_iota(jnp.int32, (8, COLS), 0)
    col = lax.broadcasted_iota(jnp.int32, (8, COLS), 1)
    zero8 = jnp.zeros((8, COLS), F32)

    mark("prep")
    dens = dens_ref[0]
    solid = des_ref[0].astype(F32) * dens
    cube = solid * solid * solid
    free_own = 1.0 - sup_ref[0].astype(F32)
    c_buf[1 + h] = cube
    free_buf[h] = free_own
    swap_out[0] = cube
    swap_out[1] = free_own
    for c in range(3):
        swap_out[2 + c] = u0_ref[other, c, 0]
        mine = u0_ref[h, c, 0]
        u0_buf[h, c] = mine
        t_buf[0, 1 + h, c, 0:ROWS] = mine * free_own
    for step in range(SWEEPS + 1):
        for n in range(4):
            for c in range(3):
                t_buf[step, n, c, ROWS : ROWS + 8] = zero8
    for n in range(2):
        for c in range(3):
            tu_buf[n, c, ROWS : ROWS + 8] = zero8
    gauss_x, gauss_y = gauss(ROWS), gauss(COLS)
    smooth_buf[...] = dot(dot(gauss_x, dens), gauss_y)
    mine8 = pl.ds(pl.multiple_of(8 * j, 8), 8)
    other8 = pl.ds(pl.multiple_of(8 * (other * LOADS_AX + l), 8), 8)
    fz_buf[0, 0, h] = smooth_buf[mine8]
    row_out[0] = smooth_buf[other8]
    row_out[1] = dens_ref[0, other8]

    @pl.loop(0, NY_ * NZ_)
    def _(i):
        dy, dz = i // NZ_, lax.rem(i, NZ_)
        offset = 16 * (lax.rem(y + dy, NY_) - y) + 2 * (z - lax.rem(z + NZ_ - dz, NZ_))
        for a in range(3):
            t = jnp.full((8, COLS), offset + (a - 1), jnp.int32).astype(F32) * (1.0 / RADIUS)
            coef_buf[i * 3 + a] = jnp.exp(-(t * t))

    mark("barrier")
    pl.semaphore_wait(barrier, RING - 1 + PLANE - 1)

    mark("sends0")
    toward = jnp.where(h == 0, below, above)
    away = jnp.where(h == 0, above, below)

    def piece(p):
        if isinstance(p, int):
            return pl.ds(p * PIECE, PIECE)
        return pl.ds(pl.multiple_of(p * PIECE, PIECE), PIECE)

    for p in range(PIECES):
        start(
            swap_out.at[:, piece(p)], swap_in.at[:, piece(p)],
            one_send.at[0], swap_recv.at[p], partner,
        )
    sent.append(whole(swap_out, one_send.at[0], swap_recv.at[0]))
    for p in range(PIECES):
        start(
            t_buf.at[0, 1 + h, :, piece(p)], t_buf.at[0, 3 * other, :, piece(p)],
            halo_send.at[0], halo_recv.at[0, p], at(toward),
        )
    got_rows = one(1, row_out, row_in, partner)

    mark("rhs")
    base = k * (2 * ROWS)
    line = lax.broadcasted_iota(jnp.int32, (2 * ROWS, CHUNK), 0)
    for n in range(2):
        for c in range(3):
            rhs_buf[n, c] = jnp.zeros((ROWS, COLS), F32)

    @pl.loop(0, POINTS // CHUNK)
    def _(i):
        cut = pl.ds(pl.multiple_of(i * CHUNK, CHUNK), CHUNK)
        node = jnp.where(h == 0, nodes_ref[0:1, cut], nodes_ref[1:2, cut])
        place = jnp.where((node >> 7) - base == line, 1.0, 0.0).astype(jnp.bfloat16)
        across = (node & 127) == line
        for c in range(3):
            force = jnp.where(h == 0, forces_ref[c, 0:1, cut], forces_ref[c, 1:2, cut])
            spread = jnp.where(across, force, 0.0)
            total = jnp.zeros((2 * ROWS, COLS), F32)
            for part in range(3):
                bits = spread.astype(jnp.bfloat16)
                total = total + lax.dot_general(
                    place, bits, (((1,), (1,)), ((), ())), preferred_element_type=F32
                )
                if part < 2:
                    spread = spread - bits.astype(F32)
            rhs_buf[0, c] += total[:ROWS]
            rhs_buf[1, c] += total[ROWS:]

    def z_send(slot, which):
        return group(slot, fz_buf.at[which], NZ_, lambda d: fz_buf.at[which, 0], z_peer)

    def z_mix(which):
        @pl.loop(0, NY_)
        def _(dy):
            for a in range(2):
                total = None
                for d in range(NZ_):
                    for b in range(2):
                        term = coef_buf[dy * (3 * NZ_) + (3 * d + a - b + 1)] * fz_buf[which, d, b]
                        total = term if total is None else total + term
                ps_buf[which, dy, a] = total

        for a in range(2):
            fy_buf[which, 0, a] = ps_buf[which, 0, a]

    def y_send(slot, which):
        return group(slot, fy_buf.at[which], NY_, lambda d: ps_buf.at[which, d], y_peer)

    def y_sum(which):
        return [
            fy_buf[which, 0, a] + fy_buf[which, 1, a] + fy_buf[which, 2, a] + fy_buf[which, 3, a]
            for a in range(2)
        ]

    def sum_of(buf, count):
        tile = buf[0]
        for d in range(1, count):
            tile = tile + buf[d]
        return tile

    mark("forward")

    @pl.loop(0, PIECES)
    def _(p):
        rows = piece(p)
        whole(swap_in.at[:, rows], one_send.at[0], swap_recv.at[p]).wait_recv()
        free = swap_in[1, rows]
        free_buf[other, rows] = free
        c_buf[1 + other, rows] = swap_in[0, rows]
        for c in range(3):
            u = swap_in[2 + c, rows]
            u0_buf[other, c, rows] = u
            t_buf[0, 1 + other, c, rows] = u * free
        start(c_buf.at[2, rows], c_buf.at[0, rows], one_send.at[2], c_recv.at[p], at(above))
        start(
            t_buf.at[0, 1 + other, :, rows], t_buf.at[0, 3 * h, :, rows],
            halo_send.at[0], halo_recv.at[0, p], at(away),
        )

    sent.append(whole(c_buf.at[0], one_send.at[2], c_recv.at[0]))
    sent.append(whole(t_buf.at[0, 1:3, :, 0:ROWS], halo_send.at[0], halo_recv.at[0, 0]))
    got_rows.wait_recv()
    fz_buf[0, 0, other] = row_in[0]
    zs = z_send(0, 0)

    has_below = jnp.where(k > 0, 1.0, 0.0)
    has_above = jnp.where(k < PLANE - 1, 1.0, 0.0)

    def wait_piece(step, p):
        if step == 0:
            whole(c_buf.at[0, piece(p)], one_send.at[2], c_recv.at[p]).wait_recv()
        whole(
            t_buf.at[step, 1:3, :, piece(p)], halo_send.at[step], halo_recv.at[step, p]
        ).wait_recv()

    def operate(step, before, finish, extra):
        def chunk(i, behind, extra):
            behind = list(behind)
            rows = pl.ds(pl.multiple_of(i * 8, 8), 8)
            after = pl.ds(pl.multiple_of(i * 8 + 8, 8), 8)
            stiff, extra = before(rows, extra)
            total = [None, None]
            lower = None
            for n in range(4):
                upper = []
                for c in range(3):
                    v, w = t_buf[step, n, c, rows], t_buf[step, n, c, after]
                    if n == 3:
                        v, w = v * has_above, w * has_above
                    upper.append(plane_modes(v, w, row, col))
                if n:
                    e = n - 1
                    f = cell_forces(cell_modes(lower, upper), stiff[e])
                    for node, sign in ((e, 1.0), (e - 1, -1.0)):
                        if not 0 <= node < 2:
                            continue
                        part = {}
                        for c in range(3):
                            for q in range(4):
                                hi = f[4 + q, c]
                                if q == 0:
                                    value = hi if sign > 0 else -hi
                                else:
                                    value = f[q, c] + hi if sign > 0 else f[q, c] - hi
                                part[c, q] = value
                        if total[node] is None:
                            total[node] = part
                        else:
                            total[node] = {key: total[node][key] + part[key] for key in part}
                lower = upper
            for node in range(2):
                for c in range(3):
                    g = []
                    for px in range(2):
                        fs, fd = total[node][c, 2 * px], total[node][c, 2 * px + 1]
                        shifted = jnp.where(col == 0, 0.0, pltpu.roll(fs + fd, 1, 1))
                        g.append(fs - fd + shifted)
                    r = pltpu.roll(g[0] + g[1], 1, 0)
                    slot = 3 * node + c
                    value = g[0] - g[1] + jnp.where(row == 0, behind[slot], r)
                    behind[slot] = r
                    extra = finish(node, c, rows, value, extra)
            return tuple(behind), extra

        def body(p, carry):
            behind, extra = carry

            @pl.when(p < PIECES - 1)
            def _():
                wait_piece(step, p + 1)

            for part in range(PIECE // 8):
                behind, extra = chunk(p * (PIECE // 8) + part, behind, extra)
            send_piece(step + 1, p)
            return behind, extra

        mark(f"wait{step}")
        wait_piece(step, 0)
        mark(f"app{step}")
        out = lax.fori_loop(0, PIECES, body, ((zero8,) * 6, extra))[1]
        return out

    def send_piece(step, p):
        rows = piece(p)
        if step < SWEEPS:
            start(
                t_buf.at[step, 2, :, rows], t_buf.at[step, 0, :, rows],
                halo_send.at[step], halo_recv.at[step, p], at(above),
            )
        start(
            t_buf.at[step, 1, :, rows], t_buf.at[step, 3, :, rows],
            halo_send.at[step], halo_recv.at[step, p], at(below),
        )

    def stiffness(rows, extra):
        acc, rolls = extra
        stiff = [STIFF_VOID + (1.0 - STIFF_VOID) * c_buf[e, rows] for e in range(3)]
        stiff[0] = stiff[0] * has_below
        out = []
        for e in range(3):
            stiff_buf[e, rows] = stiff[e]
        for n in range(2):
            b = stiff[n] + stiff[n + 1]
            b = b + jnp.where(col == 0, 0.0, pltpu.roll(b, 1, 1))
            r = pltpu.roll(b, 1, 0)
            b = b + jnp.where(row == 0, rolls[n], r)
            out.append(r)
            free = free_buf[n, rows]
            inv_buf[n, rows] = 1.0 / (free * KD * b + (1.0 - free))
        return stiff, (acc, tuple(out))

    def first(n, c, rows, value, extra):
        free, inv = free_buf[n, rows], inv_buf[n, rows]
        r = free * (rhs_buf[n, c, rows] - value) - (1.0 - free) * u0_buf[n, c, rows]
        g = r * inv
        v_buf[0, n, c, rows] = g
        t_buf[1, 1 + n, c, rows] = free * g
        return extra[0] + r * g, extra[1]

    def held(rows, extra):
        return [stiff_buf[e, rows] for e in range(3)], extra

    def later(step):
        def finish(n, c, rows, value, extra):
            free, inv = free_buf[n, rows], inv_buf[n, rows]
            v = v_buf[step - 1, n, c, rows]
            w = free * value + (1.0 - free) * v
            new = w * inv
            v_buf[step, n, c, rows] = new
            t_buf[step + 1, 1 + n, c, rows] = free * new
            return extra + v * w if step == 1 else extra

        return finish

    gr = operate(0, stiffness, first, (zero8, (zero8, zero8)))[0]
    mark("mid0")
    zs.wait_recv()
    z_mix(0)
    ys = y_send(1, 0)
    count8 = zero8
    for n in range(2):
        for i in range(ROWS // 8):
            count8 = count8 + jnp.where(c_buf[1 + n, 8 * i : 8 * i + 8] > 0.0, 1.0, 0.0)
    gw = operate(1, held, later(1), zero8)

    mark("mid1")
    sums = [jnp.sum(t, axis=0, keepdims=True) for t in (gr, gw, count8)]
    sz_buf[0] = jnp.where(row == 0, sums[0], jnp.where(row == 1, sums[1], jnp.where(row == 2, sums[2], 0.0)))
    scalar_z = group(2, sz_buf, NZ_, lambda d: sz_buf.at[0], z_peer)
    ys.wait_recv()
    denom = y_sum(0)
    for a in range(2):
        den_buf[a] = denom[a]
        fz_buf[1, 0, a] = jnp.where(c_buf[1 + a, mine8] > 0.0, 1.0, 0.0) / denom[a]
    zs = z_send(3, 1)
    operate(2, held, later(2), 0)
    mark("mid2")
    scalar_z.wait_recv()
    sy_buf[0] = sum_of(sz_buf, NZ_)
    scalar_y = group(4, sy_buf, NY_, lambda d: sy_buf.at[0], y_peer)
    zs.wait_recv()
    z_mix(1)
    ys = y_send(5, 1)
    operate(3, held, later(3), 0)
    for step in range(1, SWEEPS):
        sent.append(whole(t_buf.at[step, 1:3, :, 0:ROWS], halo_send.at[step], halo_recv.at[step, 0]))
    sent.append(whole(t_buf.at[SWEEPS, 1, :, 0:ROWS], halo_send.at[SWEEPS], halo_recv.at[SWEEPS, 0]))

    mark("q8")
    ys.wait_recv()
    q8 = y_sum(1)
    for a in range(2):
        xq_buf[0, a] = q8[a]
    xs = group(6, xq_buf, RING, lambda d: xq_buf.at[0], lambda d: ring_peer(d)[1])

    mark("combine")
    scalar_y.wait_recv()
    tile = sum_of(sy_buf, NY_)
    gr_all = jnp.sum(tile[0:1], axis=1, keepdims=True)
    gw_all = jnp.sum(tile[1:2], axis=1, keepdims=True)
    count = jnp.sum(tile[2:3], axis=1, keepdims=True)
    coefs = [jnp.broadcast_to(c, (8, COLS)) for c in chebyshev(UPPER_FACTOR * gw_all / gr_all)]

    @pl.loop(0, ROWS // 8)
    def _(i):
        rows = pl.ds(pl.multiple_of(i * 8, 8), 8)
        for n in range(2):
            free = free_buf[n, rows]
            for c in range(3):
                u = u0_buf[n, c, rows]
                for power in range(SWEEPS):
                    u = u + coefs[power] * v_buf[power, n, c, rows]
                send_buf[n, c, rows] = u
                tu_buf[n, c, rows] = free * u

    def own_layer(n, c, rows):
        return tu_buf[n, c, rows]

    def upper_layer(n, c, rows):
        if n < 2:
            return tu_buf[n, c, rows]
        u = t_buf[0, 3, c, rows]
        for power in range(SWEEPS):
            u = u + coefs[power] * t_buf[power + 1, 3, c, rows]
        return u * has_above

    def energy_chunk(e, layer, i):
        rows = pl.ds(pl.multiple_of(i * 8, 8), 8)
        after = pl.ds(pl.multiple_of(i * 8 + 8, 8), 8)
        planes = [
            [plane_modes(layer(n, c, rows), layer(n, c, after), row, col) for c in range(3)]
            for n in (e, e + 1)
        ]
        value = cell_energy(cell_modes(*planes))
        weight = (3.0 * (1.0 - STIFF_VOID)) * c_buf[1 + e, rows]
        num_buf[e, rows] = weight * value

    def smooth_xy(plane):
        return dot(gauss_x, dot(plane, gauss_y))

    mark("energy0")

    @pl.loop(0, PIECES)
    def _(p):
        for part in range(PIECE // 8):
            energy_chunk(0, own_layer, p * (PIECE // 8) + part)

    rs0 = smooth_xy(num_buf[0])
    mark("waitq")
    xs.wait_recv()
    for d in range(RING):
        there = pl.ds(pl.multiple_of(8 * lax.rem(j + RING - d, RING), 8), 8)
        for a in range(2):
            q_buf[a, there] = xq_buf[d, a]
    mark("smoothq")
    for a in range(2):
        q_buf[a] = smooth_xy(q_buf[a])
    part0 = jnp.zeros((8, COLS), F32)
    for i in range(ROWS // 8):
        cut = slice(8 * i, 8 * i + 8)
        part0 = part0 + q_buf[0, cut] * num_buf[0, cut]
    smooth_buf2 = rs0

    mark("wait_last")

    def last_piece(p):
        whole(
            t_buf.at[SWEEPS, 3, :, piece(p)], halo_send.at[SWEEPS], halo_recv.at[SWEEPS, p]
        ).wait_recv()

    last_piece(0)

    @pl.loop(0, PIECES)
    def _(p):
        @pl.when(p < PIECES - 1)
        def _():
            last_piece(p + 1)

        for part in range(PIECE // 8):
            energy_chunk(1, upper_layer, p * (PIECE // 8) + part)

    mark("smoothn")
    rs1 = smooth_xy(num_buf[1])
    part = part0
    for i in range(ROWS // 8):
        cut = slice(8 * i, 8 * i + 8)
        part = part + q_buf[1, cut] * num_buf[1, cut]
    num_buf[0] = smooth_buf2
    num_buf[1] = rs1
    for a in range(2):
        rs_buf[0, a] = num_buf[a, mine8]
    xs = group(
        7, rs_buf, RING,
        lambda d: num_buf.at[:, pl.ds(pl.multiple_of(8 * ring_peer(d)[0], 8), 8)],
        lambda d: ring_peer(d)[1],
    )
    wx_buf[0] = jnp.sum(part, axis=0, keepdims=True)
    wxs = group(8, wx_buf, RING, lambda d: wx_buf.at[0], lambda d: ring_peer(d)[1])
    got_back = one(3, send_buf.at[other], back_buf, partner)
    for c in range(3):
        disp_out[h, c, 0] = send_buf[h, c]
    mark("wait_rs")
    xs.wait_recv()
    for a in range(2):
        total = rs_buf[0, a]
        for d in range(1, RING):
            total = total + rs_buf[d, a]
        fz_buf[2, 0, a] = total
    zs = z_send(9, 2)
    mark("wait_wx")
    wxs.wait_recv()
    wz_buf[0] = sum_of(wx_buf, RING)
    wzs = group(10, wz_buf, NZ_, lambda d: wz_buf.at[0], z_peer)
    mark("wait_z")
    zs.wait_recv()
    mark("zmix2")
    z_mix(2)
    ys = y_send(11, 2)
    mark("wait_wz")
    wzs.wait_recv()
    wy_buf[0] = sum_of(wz_buf, NZ_)
    wys = group(12, wy_buf, NY_, lambda d: wy_buf.at[0], y_peer)
    mark("wait_y")
    ys.wait_recv()
    numer = y_sum(2)
    mark("wait_wy")
    wys.wait_recv()
    mark("trial")
    weighted_all = jnp.sum(sum_of(wy_buf, NY_), axis=1, keepdims=True)
    inv_mean = 1.0 / (weighted_all / count + EPSILON)
    for a in range(2):
        here = jnp.where(c_buf[1 + a, mine8] > 0.0, 1.0, 0.0)
        weighted = here * (numer[a] / den_buf[a])
        ratio = weighted * inv_mean
        old = jnp.where(h == a, dens_ref[0, mine8], row_in[1])
        trial = jnp.minimum(
            jnp.maximum(old * jnp.sqrt(ratio), old - MOVE_LIMIT), old + MOVE_LIMIT
        )
        xt_buf[0, a] = here * trial
    xs = group(13, xt_buf, RING, lambda d: xt_buf.at[0], lambda d: ring_peer(d)[1])
    mark("wait_trial")
    xs.wait_recv()
    mark("volsum")
    tile = None
    for d in range(RING):
        for a in range(2):
            tile = xt_buf[d, a] if tile is None else tile + xt_buf[d, a]
    vol_buf[0] = jnp.sum(tile, axis=0, keepdims=True)
    vs = group(14, vol_buf, PLANE, lambda i: vol_buf.at[0], plane_peer)
    mark("wait_back")
    got_back.wait_recv()
    for c in range(3):
        disp_out[other, c, 0] = back_buf[c]
    for copy in sent[:-1]:
        copy.wait_send()
    mark("wait_vol")
    vs.wait_recv()
    mark("finish")
    volume = jnp.sum(sum_of(vol_buf, PLANE), axis=1, keepdims=True)
    scale = VOLUME_TARGET / (volume / count + EPSILON)
    for d in range(RING):
        there = pl.ds(pl.multiple_of(8 * lax.rem(j + RING - d, RING), 8), 8)
        dens_out[0, there] = jnp.minimum(scale * xt_buf[d, h], 1.0)
    vs.wait_send()
    mark(None)


def shards(start_disp, density, design, support, load_nodes, load_forces):
    vmem = lambda *shape: pltpu.VMEM(shape, F32)
    dma = lambda *shape: pltpu.SemaphoreType.DMA(shape)
    plane = (ROWS, COLS)
    return pl.pallas_call(
        kernel,
        out_shape=(
            jax.ShapeDtypeStruct(start_disp.shape, F32),
            jax.ShapeDtypeStruct(density.shape, F32),
        ),
        in_specs=[pl.BlockSpec(memory_space=pltpu.VMEM)] * 6,
        out_specs=(pl.BlockSpec(memory_space=pltpu.VMEM),) * 2,
        scratch_shapes=[
            vmem(SWEEPS + 1, 4, 3, ROWS + 8, COLS),
            vmem(SWEEPS, 2, 3, *plane),
            vmem(2, 3, *plane),
            vmem(2, 3, *plane),
            vmem(3, *plane),
            vmem(3, *plane),
            vmem(2, *plane),
            vmem(2, *plane),
            vmem(5, *plane),
            vmem(5, *plane),
            vmem(2, 3, ROWS + 8, COLS),
            vmem(2, 3, *plane),
            vmem(3, *plane),
            vmem(3 * NY_ * NZ_, 8, COLS),
            vmem(2, 8, COLS),
            vmem(2, 8, COLS),
            vmem(3, NZ_, 2, 8, COLS),
            vmem(3, NY_, 2, 8, COLS),
            vmem(3, NY_, 2, 8, COLS),
            vmem(*plane),
            vmem(RING, 2, 8, COLS),
            vmem(2, *plane),
            vmem(2, *plane),
            vmem(RING, 2, 8, COLS),
            vmem(RING, 2, 8, COLS),
            vmem(2, 8, COLS),
            vmem(NZ_, 8, COLS),
            vmem(NY_, 8, COLS),
            vmem(RING, 1, COLS),
            vmem(NZ_, 1, COLS),
            vmem(NY_, 1, COLS),
            vmem(PLANE, 1, COLS),
            dma(PIECES), dma(SWEEPS + 1, PIECES), dma(PIECES), dma(SWEEPS + 1),
            dma(4), dma(4), dma(15), dma(15),
        ],
        compiler_params=pltpu.CompilerParams(
            collective_id=0, has_side_effects=True, vmem_limit_bytes=48 * 1024 * 1024
        ),
    )(start_disp, density, design, support, load_nodes, jnp.transpose(load_forces, (1, 0, 2)))


def solution(mesh):
    return jax.shard_map(
        shards,
        mesh=mesh,
        in_specs=(
            P("load", None, "slab", None, None),
            P("slab", None, None),
            P("slab", None, None),
            P("slab", None, None),
            P("load", None),
            P("load", None, None),
        ),
        out_specs=(P("load", None, "slab", None, None), P("slab", None, None)),
        check_vma=False,
    )
```

time: 80 us -> 73.2 us (0.915)
  Pallas kernels: 76.1 us -> 66.1 us
  local copies, waits for them, and re-layouts: 3.09 us -> 6 us
    pallas_call x1, Pallas kernels: 76.1 us -> 66.1 us  [shards(): pl.pallas_call(kernel, out_shape=(jax.ShapeDtypeStruct(start_disp.shape,...]
    unnamed x13 -> x14, local copies, waits for them, and re-layouts: 3.09 us -> 6 us
where the time goes in v1:
time: 73.2 us; the launch traced here: 72.7 us
  Pallas kernels  66.1 us (90%)
  local copies, waits for them, and re-layouts  6 us (8%)
    pallas_call x1, Pallas kernels, shards(): pl.pallas_call(kernel, out_shape=(jax.ShapeDtypeStruct(start_disp.shape,...  66.1 us
    unnamed x14, local copies, waits for them, and re-layouts  6 us

profile of v1, /device:TPU:1, one launch (start us, length us, event | category | flops | bytes accessed | tf_op | source)
XLA Modules:
  0.0 72.7 jit_solution(5293123934713682792)
XLA Ops:
  0.6 0.0 copy-start
  0.6 0.9 %copy-done = f32[2,3,1,64,128]{4,3,2,1,0:T(8,128)S(1)} copy-done((f32[2,3,1,64,128]{4,3,2,1,0:T(8,128)S(1)}, f32[2,3,1,64,128]{4,3,2,1,0:T(8,128)}, u32[]{:S(2)}) %copy-start) | copy-done | bytes 196632
  1.6 0.0 copy-start.1
  1.6 0.8 %copy-done.1 = f32[2,3,2048]{2,0,1:T(2,128)S(1)} copy-done((f32[2,3,2048]{2,0,1:T(2,128)S(1)}, f32[2,3,2048]{2,0,1:T(2,128)}, u32[]{:S(2)}) %copy-start.1) | copy-done | bytes 49176
  2.4 0.0 copy-start.2
  2.4 0.8 %copy-done.2 = f32[1,64,128]{2,1,0:T(8,128)S(1)} copy-done((f32[1,64,128]{2,1,0:T(8,128)S(1)}, f32[1,64,128]{2,1,0:T(8,128)}, u32[]{:S(2)}) %copy-start.2) | copy-done | bytes 32792
  3.1 0.0 copy-start.3
  3.1 0.8 %copy-done.3 = s32[1,64,128]{2,1,0:T(8,128)S(1)} copy-done((s32[1,64,128]{2,1,0:T(8,128)S(1)}, s32[1,64,128]{2,1,0:T(8,128)}, u32[]{:S(2)}) %copy-start.3) | copy-done | bytes 32792
  3.9 0.0 copy-start.4
  3.9 0.8 %copy-done.4 = s32[1,64,128]{2,1,0:T(8,128)S(1)} copy-done((s32[1,64,128]{2,1,0:T(8,128)S(1)}, s32[1,64,128]{2,1,0:T(8,128)}, u32[]{:S(2)}) %copy-start.4) | copy-done | bytes 32792
  4.6 0.0 copy-start.5
  4.6 0.7 copy-done.5
  5.4 66.1 %shard_map.77 = (f32[2,3,1,64,128]{4,3,2,1,0:T(8,128)S(1)}, f32[1,64,128]{2,1,0:T(8,128)S(1)}) custom-call(f32[2,3,1,64,128]{4,3,2,1,0:T(8,128)S(1)} %copy-done, f32[1,64,128]{2,1,0:T(8,128)S(1)} %copy-done.2, s32[1,64,128]{2,1,0:T(8,128)S(1)} %copy-done.3, s32[1,64,128]{2,1,0:T(8,128)S(1)} %copy-done.4, s32[2,2048]{1,0:T(2,128)S(1)} %copy-done.5, ...), custom_call_target="tpu_custom_call" | custom-call | tf_op jit(solution)/shard_map/pallas_call | solution.py:830
  71.4 0.7 copy.10
  72.1 0.6 copy.11
Async XLA Ops:
  0.6 0.9 %copy-start = (f32[2,3,1,64,128]{4,3,2,1,0:T(8,128)S(1)}, f32[2,3,1,64,128]{4,3,2,1,0:T(8,128)}, u32[]{:S(2)}) copy-start(f32[2,3,1,64,128]{4,3,2,1,0:T(8,128)} %u0_ref.1) | copy-start | bytes 589828
  1.6 0.8 %copy-start.1 = (f32[2,3,2048]{2,0,1:T(2,128)S(1)}, f32[2,3,2048]{2,0,1:T(2,128)}, u32[]{:S(2)}) copy-start(f32[2,3,2048]{2,0,1:T(2,128)} %param.11) | copy-start | bytes 147460
  2.4 0.8 %copy-start.2 = (f32[1,64,128]{2,1,0:T(8,128)S(1)}, f32[1,64,128]{2,1,0:T(8,128)}, u32[]{:S(2)}) copy-start(f32[1,64,128]{2,1,0:T(8,128)} %dens_ref.1) | copy-start | bytes 98308
  3.1 0.8 %copy-start.3 = (s32[1,64,128]{2,1,0:T(8,128)S(1)}, s32[1,64,128]{2,1,0:T(8,128)}, u32[]{:S(2)}) copy-start(s32[1,64,128]{2,1,0:T(8,128)} %des_ref.1) | copy-start | bytes 98308
  3.9 0.8 %copy-start.4 = (s32[1,64,128]{2,1,0:T(8,128)S(1)}, s32[1,64,128]{2,1,0:T(8,128)}, u32[]{:S(2)}) copy-start(s32[1,64,128]{2,1,0:T(8,128)} %sup_ref.1) | copy-start | bytes 98308
  4.6 0.7 copy-start.5

commit v2 on v1

--- a/solution.py
+++ b/solution.py
@@ -249,13 +249,14 @@
 
 
 def kernel(
-    u0_ref, dens_ref, des_ref, sup_ref, nodes_ref, forces_ref,
+    u0_hbm, dens_hbm, des_hbm, sup_hbm, nodes_hbm, forces_hbm,
     disp_out, dens_out,
-    t_buf, v_buf, u0_buf, rhs_buf, c_buf, stiff_buf, inv_buf, free_buf,
+    dens_ref, des_ref, sup_ref, nodes_ref, forces_ref,
+    t_buf, v_buf, u0_buf, rhs_buf, c_buf, solid_buf, stiff_buf, inv_buf, free_buf,
     swap_out, swap_in, tu_buf, send_buf, back_buf, coef_buf, row_out, row_in,
-    fz_buf, ps_buf, fy_buf, smooth_buf, xq_buf, q_buf, num_buf, rs_buf, xt_buf,
-    den_buf, sz_buf, sy_buf, wx_buf, wz_buf, wy_buf, vol_buf,
-    swap_recv, halo_recv, c_recv, halo_send, one_send, one_recv, group_send, group_recv,
+    fz_buf, ps_buf, fy_buf, smooth_buf, num_buf, num2_buf, rs_buf, xt_buf, trial_buf,
+    den_buf, sz_buf, wx_buf, wz_buf, vol_buf,
+    load_sem, swap_recv, halo_recv, c_recv, halo_send, one_send, one_recv, group_send, group_recv,
 ):
     s = lax.axis_index("slab")
     l = lax.axis_index("load")
@@ -289,6 +290,23 @@
     def plane_peer(i):
         return at(lax.rem(y + i // NZ_, NY_) * NZ_ + lax.rem(z + i % NZ_, NZ_))
 
+    loads = [
+        pltpu.make_async_copy(src, dst, load_sem.at[i])
+        for i, (src, dst) in enumerate(
+            (
+                (u0_hbm.at[other, :, 0], swap_out.at[pl.ds(2, 3)]),
+                (u0_hbm.at[h, :, 0], u0_buf.at[h]),
+                (dens_hbm, dens_ref),
+                (des_hbm, des_ref),
+                (sup_hbm, sup_ref),
+                (nodes_hbm, nodes_ref),
+                (forces_hbm, forces_ref),
+            )
+        )
+    ]
+    for copy in loads:
+        copy.start()
+
     phases = contextlib.ExitStack()
 
     def mark(name):
@@ -335,20 +353,15 @@
     col = lax.broadcasted_iota(jnp.int32, (8, COLS), 1)
     zero8 = jnp.zeros((8, COLS), F32)
 
+    @pl.loop(0, NY_ * NZ_)
+    def _(i):
+        dy, dz = i // NZ_, lax.rem(i, NZ_)
+        offset = 16 * (lax.rem(y + dy, NY_) - y) + 2 * (z - lax.rem(z + NZ_ - dz, NZ_))
+        for a in range(3):
+            t = jnp.full((8, COLS), offset + (a - 1), jnp.int32).astype(F32) * (1.0 / RADIUS)
+            coef_buf[i * 3 + a] = jnp.exp(-(t * t))
+
     mark("prep")
-    dens = dens_ref[0]
-    solid = des_ref[0].astype(F32) * dens
-    cube = solid * solid * solid
-    free_own = 1.0 - sup_ref[0].astype(F32)
-    c_buf[1 + h] = cube
-    free_buf[h] = free_own
-    swap_out[0] = cube
-    swap_out[1] = free_own
-    for c in range(3):
-        swap_out[2 + c] = u0_ref[other, c, 0]
-        mine = u0_ref[h, c, 0]
-        u0_buf[h, c] = mine
-        t_buf[0, 1 + h, c, 0:ROWS] = mine * free_own
     for step in range(SWEEPS + 1):
         for n in range(4):
             for c in range(3):
@@ -357,20 +370,24 @@
         for c in range(3):
             tu_buf[n, c, ROWS : ROWS + 8] = zero8
     gauss_x, gauss_y = gauss(ROWS), gauss(COLS)
+    for copy in loads:
+        copy.wait()
+    dens = dens_ref[0]
+    solid = des_ref[0].astype(F32) * dens
+    cube = solid * solid * solid
+    free_own = 1.0 - sup_ref[0].astype(F32)
+    c_buf[1 + h] = cube
+    free_buf[h] = free_own
+    solid_buf[h] = solid
+    swap_out[0] = solid
+    swap_out[1] = free_own
+    for c in range(3):
+        t_buf[0, 1 + h, c, 0:ROWS] = u0_buf[h, c] * free_own
     smooth_buf[...] = dot(dot(gauss_x, dens), gauss_y)
     mine8 = pl.ds(pl.multiple_of(8 * j, 8), 8)
     other8 = pl.ds(pl.multiple_of(8 * (other * LOADS_AX + l), 8), 8)
     fz_buf[0, 0, h] = smooth_buf[mine8]
-    row_out[0] = smooth_buf[other8]
-    row_out[1] = dens_ref[0, other8]
-
-    @pl.loop(0, NY_ * NZ_)
-    def _(i):
-        dy, dz = i // NZ_, lax.rem(i, NZ_)
-        offset = 16 * (lax.rem(y + dy, NY_) - y) + 2 * (z - lax.rem(z + NZ_ - dz, NZ_))
-        for a in range(3):
-            t = jnp.full((8, COLS), offset + (a - 1), jnp.int32).astype(F32) * (1.0 / RADIUS)
-            coef_buf[i * 3 + a] = jnp.exp(-(t * t))
+    row_out[...] = smooth_buf[other8]
 
     mark("barrier")
     pl.semaphore_wait(barrier, RING - 1 + PLANE - 1)
@@ -384,6 +401,7 @@
             return pl.ds(p * PIECE, PIECE)
         return pl.ds(pl.multiple_of(p * PIECE, PIECE), PIECE)
 
+    got_rows = one(1, row_out, row_in, partner)
     for p in range(PIECES):
         start(
             swap_out.at[:, piece(p)], swap_in.at[:, piece(p)],
@@ -395,7 +413,6 @@
             t_buf.at[0, 1 + h, :, piece(p)], t_buf.at[0, 3 * other, :, piece(p)],
             halo_send.at[0], halo_recv.at[0, p], at(toward),
         )
-    got_rows = one(1, row_out, row_in, partner)
 
     mark("rhs")
     base = k * (2 * ROWS)
@@ -456,6 +473,11 @@
             tile = tile + buf[d]
         return tile
 
+    mark("rows")
+    got_rows.wait_recv()
+    fz_buf[0, 0, other] = row_in[...]
+    zs = z_send(0, 0)
+
     mark("forward")
 
     @pl.loop(0, PIECES)
@@ -464,7 +486,9 @@
         whole(swap_in.at[:, rows], one_send.at[0], swap_recv.at[p]).wait_recv()
         free = swap_in[1, rows]
         free_buf[other, rows] = free
-        c_buf[1 + other, rows] = swap_in[0, rows]
+        part = swap_in[0, rows]
+        solid_buf[other, rows] = part
+        c_buf[1 + other, rows] = part * part * part
         for c in range(3):
             u = swap_in[2 + c, rows]
             u0_buf[other, c, rows] = u
@@ -477,10 +501,6 @@
 
     sent.append(whole(c_buf.at[0], one_send.at[2], c_recv.at[0]))
     sent.append(whole(t_buf.at[0, 1:3, :, 0:ROWS], halo_send.at[0], halo_recv.at[0, 0]))
-    got_rows.wait_recv()
-    fz_buf[0, 0, other] = row_in[0]
-    zs = z_send(0, 0)
-
     has_below = jnp.where(k > 0, 1.0, 0.0)
     has_above = jnp.where(k < PLANE - 1, 1.0, 0.0)
 
@@ -491,7 +511,7 @@
             t_buf.at[step, 1:3, :, piece(p)], halo_send.at[step], halo_recv.at[step, p]
         ).wait_recv()
 
-    def operate(step, before, finish, extra):
+    def operate(step, before, finish, extra, meanwhile=None):
         def chunk(i, behind, extra):
             behind = list(behind)
             rows = pl.ds(pl.multiple_of(i * 8, 8), 8)
@@ -554,6 +574,8 @@
 
         mark(f"wait{step}")
         wait_piece(step, 0)
+        if meanwhile:
+            meanwhile()
         mark(f"app{step}")
         out = lax.fori_loop(0, PIECES, body, ((zero8,) * 6, extra))[1]
         return out
@@ -618,45 +640,39 @@
     count8 = zero8
     for n in range(2):
         for i in range(ROWS // 8):
-            count8 = count8 + jnp.where(c_buf[1 + n, 8 * i : 8 * i + 8] > 0.0, 1.0, 0.0)
+            count8 = count8 + jnp.where(solid_buf[n, 8 * i : 8 * i + 8] > 0.0, 1.0, 0.0)
     gw = operate(1, held, later(1), zero8)
 
     mark("mid1")
-    sums = [jnp.sum(t, axis=0, keepdims=True) for t in (gr, gw, count8)]
-    sz_buf[0] = jnp.where(row == 0, sums[0], jnp.where(row == 1, sums[1], jnp.where(row == 2, sums[2], 0.0)))
-    scalar_z = group(2, sz_buf, NZ_, lambda d: sz_buf.at[0], z_peer)
+    lane = lax.broadcasted_iota(jnp.int32, (1, COLS), 1)
+    line0 = jnp.zeros((1, COLS), F32)
+    for i, tile in enumerate((gr, gw, count8)):
+        line0 = jnp.where(lane == i, total_of(tile), line0)
+    sz_buf[0] = line0
+    scalars = group(2, sz_buf, PLANE, lambda i: sz_buf.at[0], plane_peer)
     ys.wait_recv()
     denom = y_sum(0)
     for a in range(2):
         den_buf[a] = denom[a]
-        fz_buf[1, 0, a] = jnp.where(c_buf[1 + a, mine8] > 0.0, 1.0, 0.0) / denom[a]
+        fz_buf[1, 0, a] = jnp.where(solid_buf[a, mine8] > 0.0, 1.0, 0.0) / denom[a]
     zs = z_send(3, 1)
     operate(2, held, later(2), 0)
-    mark("mid2")
-    scalar_z.wait_recv()
-    sy_buf[0] = sum_of(sz_buf, NZ_)
-    scalar_y = group(4, sy_buf, NY_, lambda d: sy_buf.at[0], y_peer)
-    zs.wait_recv()
-    z_mix(1)
-    ys = y_send(5, 1)
-    operate(3, held, later(3), 0)
+    q_flight = []
+
+    def q_mix():
+        zs.wait_recv()
+        z_mix(1)
+        q_flight.append(y_send(5, 1))
+
+    operate(3, held, later(3), 0, q_mix)
     for step in range(1, SWEEPS):
         sent.append(whole(t_buf.at[step, 1:3, :, 0:ROWS], halo_send.at[step], halo_recv.at[step, 0]))
     sent.append(whole(t_buf.at[SWEEPS, 1, :, 0:ROWS], halo_send.at[SWEEPS], halo_recv.at[SWEEPS, 0]))
 
-    mark("q8")
-    ys.wait_recv()
-    q8 = y_sum(1)
-    for a in range(2):
-        xq_buf[0, a] = q8[a]
-    xs = group(6, xq_buf, RING, lambda d: xq_buf.at[0], lambda d: ring_peer(d)[1])
-
     mark("combine")
-    scalar_y.wait_recv()
-    tile = sum_of(sy_buf, NY_)
-    gr_all = jnp.sum(tile[0:1], axis=1, keepdims=True)
-    gw_all = jnp.sum(tile[1:2], axis=1, keepdims=True)
-    count = jnp.sum(tile[2:3], axis=1, keepdims=True)
+    scalars.wait_recv()
+    line0 = sum_of(sz_buf, PLANE)
+    gr_all, gw_all, count = line0[:, 0:1], line0[:, 1:2], line0[:, 2:3]
     coefs = [jnp.broadcast_to(c, (8, COLS)) for c in chebyshev(UPPER_FACTOR * gw_all / gr_all)]
 
     @pl.loop(0, ROWS // 8)
@@ -704,21 +720,6 @@
             energy_chunk(0, own_layer, p * (PIECE // 8) + part)
 
     rs0 = smooth_xy(num_buf[0])
-    mark("waitq")
-    xs.wait_recv()
-    for d in range(RING):
-        there = pl.ds(pl.multiple_of(8 * lax.rem(j + RING - d, RING), 8), 8)
-        for a in range(2):
-            q_buf[a, there] = xq_buf[d, a]
-    mark("smoothq")
-    for a in range(2):
-        q_buf[a] = smooth_xy(q_buf[a])
-    part0 = jnp.zeros((8, COLS), F32)
-    for i in range(ROWS // 8):
-        cut = slice(8 * i, 8 * i + 8)
-        part0 = part0 + q_buf[0, cut] * num_buf[0, cut]
-    smooth_buf2 = rs0
-
     mark("wait_last")
 
     def last_piece(p):
@@ -739,70 +740,63 @@
 
     mark("smoothn")
     rs1 = smooth_xy(num_buf[1])
-    part = part0
-    for i in range(ROWS // 8):
-        cut = slice(8 * i, 8 * i + 8)
-        part = part + q_buf[1, cut] * num_buf[1, cut]
-    num_buf[0] = smooth_buf2
-    num_buf[1] = rs1
+    num2_buf[0] = rs0
+    num2_buf[1] = rs1
     for a in range(2):
-        rs_buf[0, a] = num_buf[a, mine8]
+        rs_buf[0, a] = num2_buf[a, mine8]
     xs = group(
         7, rs_buf, RING,
-        lambda d: num_buf.at[:, pl.ds(pl.multiple_of(8 * ring_peer(d)[0], 8), 8)],
+        lambda d: num2_buf.at[:, pl.ds(pl.multiple_of(8 * ring_peer(d)[0], 8), 8)],
         lambda d: ring_peer(d)[1],
     )
-    wx_buf[0] = jnp.sum(part, axis=0, keepdims=True)
+    mark("wait_rs")
+    xs.wait_recv()
+    totals = [sum_of(rs_buf.at[:, a], RING) for a in range(2)]
+    for a in range(2):
+        fz_buf[2, 0, a] = totals[a]
+    zs = z_send(9, 2)
+    mark("wpart")
+    q_flight[0].wait_recv()
+    q8 = y_sum(1)
+    wx_buf[0] = jnp.sum(q8[0] * totals[0] + q8[1] * totals[1], axis=0, keepdims=True)
     wxs = group(8, wx_buf, RING, lambda d: wx_buf.at[0], lambda d: ring_peer(d)[1])
     got_back = one(3, send_buf.at[other], back_buf, partner)
     for c in range(3):
         disp_out[h, c, 0] = send_buf[h, c]
-    mark("wait_rs")
-    xs.wait_recv()
-    for a in range(2):
-        total = rs_buf[0, a]
-        for d in range(1, RING):
-            total = total + rs_buf[d, a]
-        fz_buf[2, 0, a] = total
-    zs = z_send(9, 2)
     mark("wait_wx")
     wxs.wait_recv()
     wz_buf[0] = sum_of(wx_buf, RING)
-    wzs = group(10, wz_buf, NZ_, lambda d: wz_buf.at[0], z_peer)
+    wzs = group(10, wz_buf, PLANE, lambda i: wz_buf.at[0], plane_peer)
     mark("wait_z")
     zs.wait_recv()
     mark("zmix2")
     z_mix(2)
     ys = y_send(11, 2)
-    mark("wait_wz")
-    wzs.wait_recv()
-    wy_buf[0] = sum_of(wz_buf, NZ_)
-    wys = group(12, wy_buf, NY_, lambda d: wy_buf.at[0], y_peer)
     mark("wait_y")
     ys.wait_recv()
     numer = y_sum(2)
-    mark("wait_wy")
-    wys.wait_recv()
+    for a in range(2):
+        here = jnp.where(solid_buf[a, mine8] > 0.0, 1.0, 0.0)
+        xt_buf[0, a] = here * (numer[a] / den_buf[a])
+    xs = group(13, xt_buf, RING, lambda d: xt_buf.at[0], lambda d: ring_peer(d)[1])
+    mark("wait_wz")
+    wzs.wait_recv()
+    weighted_all = jnp.sum(sum_of(wz_buf, PLANE), axis=1, keepdims=True)
+    inv_mean = 1.0 / (weighted_all / count + EPSILON)
+    mark("wait_x")
+    xs.wait_recv()
     mark("trial")
-    weighted_all = jnp.sum(sum_of(wy_buf, NY_), axis=1, keepdims=True)
-    inv_mean = 1.0 / (weighted_all / count + EPSILON)
-    for a in range(2):
-        here = jnp.where(c_buf[1 + a, mine8] > 0.0, 1.0, 0.0)
-        weighted = here * (numer[a] / den_buf[a])
-        ratio = weighted * inv_mean
-        old = jnp.where(h == a, dens_ref[0, mine8], row_in[1])
-        trial = jnp.minimum(
-            jnp.maximum(old * jnp.sqrt(ratio), old - MOVE_LIMIT), old + MOVE_LIMIT
-        )
-        xt_buf[0, a] = here * trial
-    xs = group(13, xt_buf, RING, lambda d: xt_buf.at[0], lambda d: ring_peer(d)[1])
-    mark("wait_trial")
-    xs.wait_recv()
-    mark("volsum")
-    tile = None
+    tile = zero8
     for d in range(RING):
+        there = pl.ds(pl.multiple_of(8 * lax.rem(j + RING - d, RING), 8), 8)
         for a in range(2):
-            tile = xt_buf[d, a] if tile is None else tile + xt_buf[d, a]
+            old = solid_buf[a, there]
+            trial = jnp.minimum(
+                jnp.maximum(old * jnp.sqrt(xt_buf[d, a] * inv_mean), old - MOVE_LIMIT),
+                old + MOVE_LIMIT,
+            )
+            tile = tile + trial
+            trial_buf[a, there] = trial
     vol_buf[0] = jnp.sum(tile, axis=0, keepdims=True)
     vs = group(14, vol_buf, PLANE, lambda i: vol_buf.at[0], plane_peer)
     mark("wait_back")
@@ -816,31 +810,38 @@
     mark("finish")
     volume = jnp.sum(sum_of(vol_buf, PLANE), axis=1, keepdims=True)
     scale = VOLUME_TARGET / (volume / count + EPSILON)
-    for d in range(RING):
-        there = pl.ds(pl.multiple_of(8 * lax.rem(j + RING - d, RING), 8), 8)
-        dens_out[0, there] = jnp.minimum(scale * xt_buf[d, h], 1.0)
+    dens_out[0] = jnp.minimum(scale * trial_buf[h], 1.0)
     vs.wait_send()
     mark(None)
 
 
 def shards(start_disp, density, design, support, load_nodes, load_forces):
+    arrays = (
+        start_disp, density, design, support, load_nodes, jnp.transpose(load_forces, (1, 0, 2)),
+    )
     vmem = lambda *shape: pltpu.VMEM(shape, F32)
     dma = lambda *shape: pltpu.SemaphoreType.DMA(shape)
     plane = (ROWS, COLS)
     return pl.pallas_call(
         kernel,
         out_shape=(
-            jax.ShapeDtypeStruct(start_disp.shape, F32),
-            jax.ShapeDtypeStruct(density.shape, F32),
+            pltpu.VMEM(start_disp.shape, F32),
+            pltpu.VMEM(density.shape, F32),
         ),
-        in_specs=[pl.BlockSpec(memory_space=pltpu.VMEM)] * 6,
+        in_specs=[pl.BlockSpec(memory_space=pltpu.HBM)] * 6,
         out_specs=(pl.BlockSpec(memory_space=pltpu.VMEM),) * 2,
         scratch_shapes=[
+            vmem(1, *plane),
+            pltpu.VMEM((1, *plane), jnp.int32),
+            pltpu.VMEM((1, *plane), jnp.int32),
+            pltpu.VMEM((2, POINTS), jnp.int32),
+            vmem(3, 2, POINTS),
             vmem(SWEEPS + 1, 4, 3, ROWS + 8, COLS),
             vmem(SWEEPS, 2, 3, *plane),
             vmem(2, 3, *plane),
             vmem(2, 3, *plane),
             vmem(3, *plane),
+            vmem(2, *plane),
             vmem(3, *plane),
             vmem(2, *plane),
             vmem(2, *plane),
@@ -850,31 +851,29 @@
             vmem(2, 3, *plane),
             vmem(3, *plane),
             vmem(3 * NY_ * NZ_, 8, COLS),
-            vmem(2, 8, COLS),
-            vmem(2, 8, COLS),
+            vmem(8, COLS),
+            vmem(8, COLS),
             vmem(3, NZ_, 2, 8, COLS),
             vmem(3, NY_, 2, 8, COLS),
             vmem(3, NY_, 2, 8, COLS),
             vmem(*plane),
-            vmem(RING, 2, 8, COLS),
             vmem(2, *plane),
             vmem(2, *plane),
             vmem(RING, 2, 8, COLS),
             vmem(RING, 2, 8, COLS),
+            vmem(2, *plane),
             vmem(2, 8, COLS),
-            vmem(NZ_, 8, COLS),
-            vmem(NY_, 8, COLS),
+            vmem(PLANE, 1, COLS),
             vmem(RING, 1, COLS),
-            vmem(NZ_, 1, COLS),
-            vmem(NY_, 1, COLS),
             vmem(PLANE, 1, COLS),
-            dma(PIECES), dma(SWEEPS + 1, PIECES), dma(PIECES), dma(SWEEPS + 1),
+            vmem(PLANE, 1, COLS),
+            dma(7), dma(PIECES), dma(SWEEPS + 1, PIECES), dma(PIECES), dma(SWEEPS + 1),
             dma(4), dma(4), dma(15), dma(15),
         ],
         compiler_params=pltpu.CompilerParams(
             collective_id=0, has_side_effects=True, vmem_limit_bytes=48 * 1024 * 1024
         ),
-    )(start_disp, density, design, support, load_nodes, jnp.transpose(load_forces, (1, 0, 2)))
+    )(*(pltpu.with_memory_space_constraint(a, pltpu.HBM) for a in arrays))
 
 
 def solution(mesh):

time: 73.2 us -> 66 us (0.902)
  local copies, waits for them, and re-layouts: 6 us -> 1.29 us
  Pallas kernels: 66.1 us -> 64 us
    unnamed x14 -> x2, local copies, waits for them, and re-layouts: 6 us -> 1.29 us
    pallas_call x1, Pallas kernels: 66.1 us -> 64 us  [shards(): pl.pallas_call(kernel, out_shape=(pltpu.VMEM(start_disp.shape, F32), pltp...]
where the time goes in v2:
time: 66 us
  Pallas kernels  64 us (97%)
  local copies, waits for them, and re-layouts  1.29 us (2%)
    pallas_call x1, Pallas kernels, shards(): pl.pallas_call(kernel, out_shape=(pltpu.VMEM(start_disp.shape, F32), pltp...  64 us

profile of v2, /device:TPU:1, one launch (start us, length us, event | category | flops | bytes accessed | tf_op | source)
XLA Modules:
  0.0 66.0 jit_solution(12063921820435240063)
XLA Ops:
  0.6 64.0 %shard_map.77 = (f32[2,3,1,64,128]{4,3,2,1,0:T(8,128)S(1)}, f32[1,64,128]{2,1,0:T(8,128)S(1)}) custom-call(f32[2,3,1,64,128]{4,3,2,1,0:T(8,128)} %u0_hbm.1, f32[1,64,128]{2,1,0:T(8,128)} %dens_hbm.1, s32[1,64,128]{2,1,0:T(8,128)} %des_hbm.1, s32[1,64,128]{2,1,0:T(8,128)} %sup_hbm.1, s32[2,2048]{1,0:T(2,128)} %nodes_hbm.1, f32[3,2,2048]{2,1,0:T(2,128)} %bitcast.1), custom_call_target="tpu_custom_call" | custom-call | tf_op jit(solution)/shard_map/pallas_call | solution.py:825
  64.7 0.7 %copy.10 = f32[2,3,1,64,128]{4,3,2,1,0:T(8,128)} copy(f32[2,3,1,64,128]{4,3,2,1,0:T(8,128)S(1)} %get-tuple-element.2) | data formatting | bytes 393216
  65.3 0.6 copy.11

commit v3 on v2

--- a/solution.py
+++ b/solution.py
@@ -28,8 +28,7 @@
 ROWS, COLS = 64, 128
 POINTS = 2048
 CHUNK = 256
-PIECE = 16
-PIECES = ROWS // PIECE
+PIECES = 5
 
 
 def hex_stiffness():
@@ -369,7 +368,17 @@
     for n in range(2):
         for c in range(3):
             tu_buf[n, c, ROWS : ROWS + 8] = zero8
-    gauss_x, gauss_y = gauss(ROWS), gauss(COLS)
+    @pl.when(k == 0)
+    def _():
+        c_buf[0] = jnp.zeros((ROWS, COLS), F32)
+        for step in range(SWEEPS):
+            t_buf[step, 0, :, 0:ROWS] = jnp.zeros((3, ROWS, COLS), F32)
+
+    @pl.when(k == PLANE - 1)
+    def _():
+        for step in range(SWEEPS + 1):
+            t_buf[step, 3, :, 0:ROWS] = jnp.zeros((3, ROWS, COLS), F32)
+
     for copy in loads:
         copy.wait()
     dens = dens_ref[0]
@@ -383,12 +392,6 @@
     swap_out[1] = free_own
     for c in range(3):
         t_buf[0, 1 + h, c, 0:ROWS] = u0_buf[h, c] * free_own
-    smooth_buf[...] = dot(dot(gauss_x, dens), gauss_y)
-    mine8 = pl.ds(pl.multiple_of(8 * j, 8), 8)
-    other8 = pl.ds(pl.multiple_of(8 * (other * LOADS_AX + l), 8), 8)
-    fz_buf[0, 0, h] = smooth_buf[mine8]
-    row_out[...] = smooth_buf[other8]
-
     mark("barrier")
     pl.semaphore_wait(barrier, RING - 1 + PLANE - 1)
 
@@ -396,23 +399,41 @@
     toward = jnp.where(h == 0, below, above)
     away = jnp.where(h == 0, above, below)
 
+    inside = jnp.logical_and(k > 0, k < PLANE - 1)
+
     def piece(p):
         if isinstance(p, int):
-            return pl.ds(p * PIECE, PIECE)
-        return pl.ds(pl.multiple_of(p * PIECE, PIECE), PIECE)
-
-    got_rows = one(1, row_out, row_in, partner)
+            return pl.ds(8 * p, 8) if p < 2 else pl.ds(16 * p - 16, 16)
+        return pl.ds(pl.multiple_of(16 * p - 16, 16), 16)
+
+    def each_piece(do):
+        do(0)
+        do(1)
+        pl.loop(2, PIECES)(do)
+
     for p in range(PIECES):
         start(
             swap_out.at[:, piece(p)], swap_in.at[:, piece(p)],
             one_send.at[0], swap_recv.at[p], partner,
         )
     sent.append(whole(swap_out, one_send.at[0], swap_recv.at[0]))
-    for p in range(PIECES):
-        start(
-            t_buf.at[0, 1 + h, :, piece(p)], t_buf.at[0, 3 * other, :, piece(p)],
-            halo_send.at[0], halo_recv.at[0, p], at(toward),
-        )
+
+    @pl.when(jnp.where(h == 0, k > 0, k < PLANE - 1))
+    def _():
+        for p in range(PIECES):
+            start(
+                t_buf.at[0, 1 + h, :, piece(p)], t_buf.at[0, 3 * other, :, piece(p)],
+                halo_send.at[0], halo_recv.at[0, p], at(toward),
+            )
+
+    mark("smooth")
+    gauss_x, gauss_y = gauss(ROWS), gauss(COLS)
+    smooth_buf[...] = dot(dot(gauss_x, dens), gauss_y)
+    mine8 = pl.ds(pl.multiple_of(8 * j, 8), 8)
+    other8 = pl.ds(pl.multiple_of(8 * (other * LOADS_AX + l), 8), 8)
+    fz_buf[0, 0, h] = smooth_buf[mine8]
+    row_out[...] = smooth_buf[other8]
+    got_rows = one(1, row_out, row_in, partner)
 
     mark("rhs")
     base = k * (2 * ROWS)
@@ -480,8 +501,9 @@
 
     mark("forward")
 
-    @pl.loop(0, PIECES)
-    def _(p):
+    has_away = jnp.where(h == 0, k < PLANE - 1, k > 0)
+
+    def forward(p):
         rows = piece(p)
         whole(swap_in.at[:, rows], one_send.at[0], swap_recv.at[p]).wait_recv()
         free = swap_in[1, rows]
@@ -493,29 +515,46 @@
             u = swap_in[2 + c, rows]
             u0_buf[other, c, rows] = u
             t_buf[0, 1 + other, c, rows] = u * free
-        start(c_buf.at[2, rows], c_buf.at[0, rows], one_send.at[2], c_recv.at[p], at(above))
-        start(
-            t_buf.at[0, 1 + other, :, rows], t_buf.at[0, 3 * h, :, rows],
-            halo_send.at[0], halo_recv.at[0, p], at(away),
-        )
-
-    sent.append(whole(c_buf.at[0], one_send.at[2], c_recv.at[0]))
-    sent.append(whole(t_buf.at[0, 1:3, :, 0:ROWS], halo_send.at[0], halo_recv.at[0, 0]))
+
+        @pl.when(has_away)
+        def _():
+            start(
+                t_buf.at[0, 1 + other, :, rows], t_buf.at[0, 3 * h, :, rows],
+                halo_send.at[0], halo_recv.at[0, p], at(away),
+            )
+
+        @pl.when(k < PLANE - 1)
+        def _():
+            start(c_buf.at[2, rows], c_buf.at[0, rows], one_send.at[2], c_recv.at[p], at(above))
+
+    each_piece(forward)
     has_below = jnp.where(k > 0, 1.0, 0.0)
-    has_above = jnp.where(k < PLANE - 1, 1.0, 0.0)
-
     def wait_piece(step, p):
+        rows = piece(p)
         if step == 0:
-            whole(c_buf.at[0, piece(p)], one_send.at[2], c_recv.at[p]).wait_recv()
-        whole(
-            t_buf.at[step, 1:3, :, piece(p)], halo_send.at[step], halo_recv.at[step, p]
-        ).wait_recv()
+            @pl.when(k > 0)
+            def _():
+                whole(c_buf.at[0, rows], one_send.at[2], c_recv.at[p]).wait_recv()
+
+        @pl.when(inside)
+        def _():
+            whole(
+                t_buf.at[step, 1:3, :, rows], halo_send.at[step], halo_recv.at[step, p]
+            ).wait_recv()
+
+        @pl.when(jnp.logical_not(inside))
+        def _():
+            whole(
+                t_buf.at[step, 1, :, rows], halo_send.at[step], halo_recv.at[step, p]
+            ).wait_recv()
+
+    def chunk_rows(i):
+        return pl.ds(8 * i, 8) if isinstance(i, int) else pl.ds(pl.multiple_of(i * 8, 8), 8)
 
     def operate(step, before, finish, extra, meanwhile=None):
         def chunk(i, behind, extra):
             behind = list(behind)
-            rows = pl.ds(pl.multiple_of(i * 8, 8), 8)
-            after = pl.ds(pl.multiple_of(i * 8 + 8, 8), 8)
+            rows, after = chunk_rows(i), chunk_rows(i + 1)
             stiff, extra = before(rows, extra)
             total = [None, None]
             lower = None
@@ -523,8 +562,6 @@
                 upper = []
                 for c in range(3):
                     v, w = t_buf[step, n, c, rows], t_buf[step, n, c, after]
-                    if n == 3:
-                        v, w = v * has_above, w * has_above
                     upper.append(plane_modes(v, w, row, col))
                 if n:
                     e = n - 1
@@ -567,8 +604,8 @@
             def _():
                 wait_piece(step, p + 1)
 
-            for part in range(PIECE // 8):
-                behind, extra = chunk(p * (PIECE // 8) + part, behind, extra)
+            for part in range(2):
+                behind, extra = chunk(2 * p - 2 + part, behind, extra)
             send_piece(step + 1, p)
             return behind, extra
 
@@ -577,20 +614,29 @@
         if meanwhile:
             meanwhile()
         mark(f"app{step}")
-        out = lax.fori_loop(0, PIECES, body, ((zero8,) * 6, extra))[1]
-        return out
+        behind = (zero8,) * 6
+        for p in range(2):
+            wait_piece(step, p + 1)
+            behind, extra = chunk(p, behind, extra)
+            send_piece(step + 1, p)
+        return lax.fori_loop(2, PIECES, body, (behind, extra))[1]
 
     def send_piece(step, p):
         rows = piece(p)
         if step < SWEEPS:
+            @pl.when(k < PLANE - 1)
+            def _():
+                start(
+                    t_buf.at[step, 2, :, rows], t_buf.at[step, 0, :, rows],
+                    halo_send.at[step], halo_recv.at[step, p], at(above),
+                )
+
+        @pl.when(k > 0)
+        def _():
             start(
-                t_buf.at[step, 2, :, rows], t_buf.at[step, 0, :, rows],
-                halo_send.at[step], halo_recv.at[step, p], at(above),
+                t_buf.at[step, 1, :, rows], t_buf.at[step, 3, :, rows],
+                halo_send.at[step], halo_recv.at[step, p], at(below),
             )
-        start(
-            t_buf.at[step, 1, :, rows], t_buf.at[step, 3, :, rows],
-            halo_send.at[step], halo_recv.at[step, p], at(below),
-        )
 
     def stiffness(rows, extra):
         acc, rolls = extra
@@ -665,10 +711,6 @@
         q_flight.append(y_send(5, 1))
 
     operate(3, held, later(3), 0, q_mix)
-    for step in range(1, SWEEPS):
-        sent.append(whole(t_buf.at[step, 1:3, :, 0:ROWS], halo_send.at[step], halo_recv.at[step, 0]))
-    sent.append(whole(t_buf.at[SWEEPS, 1, :, 0:ROWS], halo_send.at[SWEEPS], halo_recv.at[SWEEPS, 0]))
-
     mark("combine")
     scalars.wait_recv()
     line0 = sum_of(sz_buf, PLANE)
@@ -696,11 +738,10 @@
         u = t_buf[0, 3, c, rows]
         for power in range(SWEEPS):
             u = u + coefs[power] * t_buf[power + 1, 3, c, rows]
-        return u * has_above
+        return u
 
     def energy_chunk(e, layer, i):
-        rows = pl.ds(pl.multiple_of(i * 8, 8), 8)
-        after = pl.ds(pl.multiple_of(i * 8 + 8, 8), 8)
+        rows, after = chunk_rows(i), chunk_rows(i + 1)
         planes = [
             [plane_modes(layer(n, c, rows), layer(n, c, after), row, col) for c in range(3)]
             for n in (e, e + 1)
@@ -714,29 +755,34 @@
 
     mark("energy0")
 
-    @pl.loop(0, PIECES)
+    @pl.loop(0, ROWS // 16)
     def _(p):
-        for part in range(PIECE // 8):
-            energy_chunk(0, own_layer, p * (PIECE // 8) + part)
+        for part in range(2):
+            energy_chunk(0, own_layer, 2 * p + part)
 
     rs0 = smooth_xy(num_buf[0])
     mark("wait_last")
 
     def last_piece(p):
-        whole(
-            t_buf.at[SWEEPS, 3, :, piece(p)], halo_send.at[SWEEPS], halo_recv.at[SWEEPS, p]
-        ).wait_recv()
+        @pl.when(k < PLANE - 1)
+        def _():
+            whole(
+                t_buf.at[SWEEPS, 3, :, piece(p)], halo_send.at[SWEEPS], halo_recv.at[SWEEPS, p]
+            ).wait_recv()
 
     last_piece(0)
-
-    @pl.loop(0, PIECES)
+    for p in range(2):
+        last_piece(p + 1)
+        energy_chunk(1, upper_layer, p)
+
+    @pl.loop(2, PIECES)
     def _(p):
         @pl.when(p < PIECES - 1)
         def _():
             last_piece(p + 1)
 
-        for part in range(PIECE // 8):
-            energy_chunk(1, upper_layer, p * (PIECE // 8) + part)
+        for part in range(2):
+            energy_chunk(1, upper_layer, 2 * p - 2 + part)
 
     mark("smoothn")
     rs1 = smooth_xy(num_buf[1])
@@ -754,7 +800,7 @@
     totals = [sum_of(rs_buf.at[:, a], RING) for a in range(2)]
     for a in range(2):
         fz_buf[2, 0, a] = totals[a]
-    zs = z_send(9, 2)
+    zs = z_send(4, 2)
     mark("wpart")
     q_flight[0].wait_recv()
     q8 = y_sum(1)
@@ -766,19 +812,19 @@
     mark("wait_wx")
     wxs.wait_recv()
     wz_buf[0] = sum_of(wx_buf, RING)
-    wzs = group(10, wz_buf, PLANE, lambda i: wz_buf.at[0], plane_peer)
+    wzs = group(9, wz_buf, PLANE, lambda i: wz_buf.at[0], plane_peer)
     mark("wait_z")
     zs.wait_recv()
     mark("zmix2")
     z_mix(2)
-    ys = y_send(11, 2)
+    ys = y_send(6, 2)
     mark("wait_y")
     ys.wait_recv()
     numer = y_sum(2)
     for a in range(2):
         here = jnp.where(solid_buf[a, mine8] > 0.0, 1.0, 0.0)
         xt_buf[0, a] = here * (numer[a] / den_buf[a])
-    xs = group(13, xt_buf, RING, lambda d: xt_buf.at[0], lambda d: ring_peer(d)[1])
+    xs = group(10, xt_buf, RING, lambda d: xt_buf.at[0], lambda d: ring_peer(d)[1])
     mark("wait_wz")
     wzs.wait_recv()
     weighted_all = jnp.sum(sum_of(wz_buf, PLANE), axis=1, keepdims=True)
@@ -798,13 +844,24 @@
             tile = tile + trial
             trial_buf[a, there] = trial
     vol_buf[0] = jnp.sum(tile, axis=0, keepdims=True)
-    vs = group(14, vol_buf, PLANE, lambda i: vol_buf.at[0], plane_peer)
+    vs = group(11, vol_buf, PLANE, lambda i: vol_buf.at[0], plane_peer)
     mark("wait_back")
     got_back.wait_recv()
     for c in range(3):
         disp_out[other, c, 0] = back_buf[c]
     for copy in sent[:-1]:
         copy.wait_send()
+
+    def layers_sent(step, layers):
+        whole(
+            t_buf.at[step, layers, :, 0:ROWS], halo_send.at[step], halo_recv.at[step, 0]
+        ).wait_send()
+
+    for step in range(SWEEPS):
+        pl.when(inside)(lambda: layers_sent(step, pl.ds(1, 2)))
+        pl.when(jnp.logical_not(inside))(lambda: layers_sent(step, 1))
+    pl.when(k > 0)(lambda: layers_sent(SWEEPS, 1))
+    pl.when(k < PLANE - 1)(lambda: whole(c_buf.at[0], one_send.at[2], c_recv.at[0]).wait_send())
     mark("wait_vol")
     vs.wait_recv()
     mark("finish")
@@ -868,7 +925,7 @@
             vmem(PLANE, 1, COLS),
             vmem(PLANE, 1, COLS),
             dma(7), dma(PIECES), dma(SWEEPS + 1, PIECES), dma(PIECES), dma(SWEEPS + 1),
-            dma(4), dma(4), dma(15), dma(15),
+            dma(4), dma(4), dma(12), dma(12),
         ],
         compiler_params=pltpu.CompilerParams(
             collective_id=0, has_side_effects=True, vmem_limit_bytes=48 * 1024 * 1024

time: 66 us -> 65.8 us (level)
  no operation moved by 1% of the time
where the time goes in v3:
time: 65.8 us
  Pallas kernels  63.8 us (97%)
  local copies, waits for them, and re-layouts  1.29 us (2%)
    pallas_call x1, Pallas kernels, shards(): pl.pallas_call(kernel, out_shape=(pltpu.VMEM(start_disp.shape, F32), pltp...  63.8 us

profile of v3, /device:TPU:1, one launch (start us, length us, event | category | flops | bytes accessed | tf_op | source)
XLA Modules:
  0.0 65.8 jit_solution(3348321351735000769)
XLA Ops:
  0.6 63.8 %shard_map.77 = (f32[2,3,1,64,128]{4,3,2,1,0:T(8,128)S(1)}, f32[1,64,128]{2,1,0:T(8,128)S(1)}) custom-call(f32[2,3,1,64,128]{4,3,2,1,0:T(8,128)} %u0_hbm.1, f32[1,64,128]{2,1,0:T(8,128)} %dens_hbm.1, s32[1,64,128]{2,1,0:T(8,128)} %des_hbm.1, s32[1,64,128]{2,1,0:T(8,128)} %sup_hbm.1, s32[2,2048]{1,0:T(2,128)} %nodes_hbm.1, f32[3,2,2048]{2,1,0:T(2,128)} %bitcast.1), custom_call_target="tpu_custom_call" | custom-call | tf_op jit(solution)/shard_map/pallas_call | solution.py:882
  64.5 0.7 %copy.10 = f32[2,3,1,64,128]{4,3,2,1,0:T(8,128)} copy(f32[2,3,1,64,128]{4,3,2,1,0:T(8,128)S(1)} %get-tuple-element.2) | data formatting | bytes 393216
  65.1 0.6 copy.11

commit v4 on v3

--- a/solution.py
+++ b/solution.py
@@ -255,7 +255,7 @@
     swap_out, swap_in, tu_buf, send_buf, back_buf, coef_buf, row_out, row_in,
     fz_buf, ps_buf, fy_buf, smooth_buf, num_buf, num2_buf, rs_buf, xt_buf, trial_buf,
     den_buf, sz_buf, wx_buf, wz_buf, vol_buf,
-    load_sem, swap_recv, halo_recv, c_recv, halo_send, one_send, one_recv, group_send, group_recv,
+    heard, load_sem, swap_recv, halo_recv, c_recv, halo_send, one_send, one_recv, group_send, group_recv,
 ):
     s = lax.axis_index("slab")
     l = lax.axis_index("load")
@@ -315,10 +315,12 @@
 
     mark("signals")
     barrier = pltpu.get_barrier_semaphore()
-    for d in range(1, RING):
-        pl.semaphore_signal(barrier, inc=1, device_id=ring_peer(d)[1], device_id_type=MESH)
-    for i in range(1, PLANE):
-        pl.semaphore_signal(barrier, inc=1, device_id=plane_peer(i), device_id_type=MESH)
+    near = [ring_peer(d)[1] for d in range(1, RING)]
+    near += [y_peer(d) for d in range(1, NY_)]
+    near += [z_peer(d) for d in (1, 2, NZ_ - 2, NZ_ - 1)]
+    near += [at(above), at(below)]
+    for device in near:
+        pl.semaphore_signal(barrier, inc=1, device_id=device, device_id_type=MESH)
 
     sent = []
 
@@ -351,14 +353,6 @@
     row = lax.broadcasted_iota(jnp.int32, (8, COLS), 0)
     col = lax.broadcasted_iota(jnp.int32, (8, COLS), 1)
     zero8 = jnp.zeros((8, COLS), F32)
-
-    @pl.loop(0, NY_ * NZ_)
-    def _(i):
-        dy, dz = i // NZ_, lax.rem(i, NZ_)
-        offset = 16 * (lax.rem(y + dy, NY_) - y) + 2 * (z - lax.rem(z + NZ_ - dz, NZ_))
-        for a in range(3):
-            t = jnp.full((8, COLS), offset + (a - 1), jnp.int32).astype(F32) * (1.0 / RADIUS)
-            coef_buf[i * 3 + a] = jnp.exp(-(t * t))
 
     mark("prep")
     for step in range(SWEEPS + 1):
@@ -393,7 +387,9 @@
     for c in range(3):
         t_buf[0, 1 + h, c, 0:ROWS] = u0_buf[h, c] * free_own
     mark("barrier")
-    pl.semaphore_wait(barrier, RING - 1 + PLANE - 1)
+    pl.semaphore_wait(barrier, len(near))
+    for d in (2, NZ_ - 2):
+        pl.semaphore_signal(heard.at[0], inc=1, device_id=z_peer(d), device_id_type=MESH)
 
     mark("sends0")
     toward = jnp.where(h == 0, below, above)
@@ -434,6 +430,15 @@
     fz_buf[0, 0, h] = smooth_buf[mine8]
     row_out[...] = smooth_buf[other8]
     got_rows = one(1, row_out, row_in, partner)
+
+    mark("coef")
+    @pl.loop(0, NY_ * NZ_)
+    def _(i):
+        dy, dz = i // NZ_, lax.rem(i, NZ_)
+        offset = 16 * (lax.rem(y + dy, NY_) - y) + 2 * (z - lax.rem(z + NZ_ - dz, NZ_))
+        for a in range(3):
+            t = jnp.full((8, COLS), offset + (a - 1), jnp.int32).astype(F32) * (1.0 / RADIUS)
+            coef_buf[i * 3 + a] = jnp.exp(-(t * t))
 
     mark("rhs")
     base = k * (2 * ROWS)
@@ -495,6 +500,9 @@
         return tile
 
     mark("rows")
+    pl.semaphore_wait(heard.at[0], 2)
+    for d in range(1, NY_):
+        pl.semaphore_signal(heard.at[1], inc=1, device_id=y_peer(d), device_id_type=MESH)
     got_rows.wait_recv()
     fz_buf[0, 0, other] = row_in[...]
     zs = z_send(0, 0)
@@ -692,6 +700,7 @@
     mark("mid1")
     lane = lax.broadcasted_iota(jnp.int32, (1, COLS), 1)
     line0 = jnp.zeros((1, COLS), F32)
+    pl.semaphore_wait(heard.at[1], NY_ - 1)
     for i, tile in enumerate((gr, gw, count8)):
         line0 = jnp.where(lane == i, total_of(tile), line0)
     sz_buf[0] = line0
@@ -872,6 +881,17 @@
     mark(None)
 
 
+def put_out(disp_ref, dens_ref, disp_out, dens_out, sems):
+    copies = [
+        pltpu.make_async_copy(disp_ref, disp_out, sems.at[0]),
+        pltpu.make_async_copy(dens_ref, dens_out, sems.at[1]),
+    ]
+    for copy in copies:
+        copy.start()
+    for copy in copies:
+        copy.wait()
+
+
 def shards(start_disp, density, design, support, load_nodes, load_forces):
     arrays = (
         start_disp, density, design, support, load_nodes, jnp.transpose(load_forces, (1, 0, 2)),
@@ -879,7 +899,7 @@
     vmem = lambda *shape: pltpu.VMEM(shape, F32)
     dma = lambda *shape: pltpu.SemaphoreType.DMA(shape)
     plane = (ROWS, COLS)
-    return pl.pallas_call(
+    results = pl.pallas_call(
         kernel,
         out_shape=(
             pltpu.VMEM(start_disp.shape, F32),
@@ -924,13 +944,23 @@
             vmem(RING, 1, COLS),
             vmem(PLANE, 1, COLS),
             vmem(PLANE, 1, COLS),
-            dma(7), dma(PIECES), dma(SWEEPS + 1, PIECES), dma(PIECES), dma(SWEEPS + 1),
+            pltpu.SemaphoreType.REGULAR((2,)), dma(7), dma(PIECES), dma(SWEEPS + 1, PIECES), dma(PIECES), dma(SWEEPS + 1),
             dma(4), dma(4), dma(12), dma(12),
         ],
         compiler_params=pltpu.CompilerParams(
             collective_id=0, has_side_effects=True, vmem_limit_bytes=48 * 1024 * 1024
         ),
     )(*(pltpu.with_memory_space_constraint(a, pltpu.HBM) for a in arrays))
+    return pl.pallas_call(
+        put_out,
+        out_shape=(
+            pltpu.HBM(start_disp.shape, F32),
+            pltpu.HBM(density.shape, F32),
+        ),
+        in_specs=[pl.BlockSpec(memory_space=pltpu.VMEM)] * 2,
+        out_specs=(pl.BlockSpec(memory_space=pltpu.HBM),) * 2,
+        scratch_shapes=[dma(2)],
+    )(*(pltpu.with_memory_space_constraint(a, pltpu.VMEM) for a in results))
 
 
 def solution(mesh):

time: 65.8 us -> 63.8 us (0.970)
  local copies, waits for them, and re-layouts: 1.29 us -> 0 us
  Pallas kernels: 63.8 us -> 63.1 us
    pallas_call x1, Pallas kernels: 63.8 us -> 62.4 us  [shards(): pl.pallas_call(kernel, out_shape=(pltpu.VMEM(start_disp.shape, F32), pltp...]
    unnamed x2 -> x0, local copies, waits for them, and re-layouts: 1.29 us -> none
    pallas_call x0 -> x1, Pallas kernels: none -> 0.7 us  [shards(): pl.pallas_call(put_out, out_shape=(pltpu.HBM(start_disp.shape, F32), pltp...]
where the time goes in v4:
time: 63.8 us; the launch traced here: 63.7 us
  Pallas kernels  63.1 us (99%)
  between operations  0.64 us (1%)
    pallas_call x1, Pallas kernels, shards(): pl.pallas_call(kernel, out_shape=(pltpu.VMEM(start_disp.shape, F32), pltp...  62.4 us

profile of v4, /device:TPU:1, one launch (start us, length us, event | category | flops | bytes accessed | tf_op | source)
XLA Modules:
  0.0 63.7 jit_solution(12586820790594557390)
XLA Ops:
  0.6 62.4 %shard_map.77 = (f32[2,3,1,64,128]{4,3,2,1,0:T(8,128)S(1)}, f32[1,64,128]{2,1,0:T(8,128)S(1)}) custom-call(f32[2,3,1,64,128]{4,3,2,1,0:T(8,128)} %u0_hbm.1, f32[1,64,128]{2,1,0:T(8,128)} %dens_hbm.1, s32[1,64,128]{2,1,0:T(8,128)} %des_hbm.1, s32[1,64,128]{2,1,0:T(8,128)} %sup_hbm.1, s32[2,2048]{1,0:T(2,128)} %nodes_hbm.1, f32[3,2,2048]{2,1,0:T(2,128)} %bitcast.1), custom_call_target="tpu_custom_call" | custom-call | tf_op jit(solution)/shard_map/pallas_call | solution.py:902
  63.0 0.7 %shard_map.78 = (f32[2,3,1,64,128]{4,3,2,1,0:T(8,128)}, f32[1,64,128]{2,1,0:T(8,128)}) custom-call(f32[2,3,1,64,128]{4,3,2,1,0:T(8,128)S(1)} %get-tuple-element.4.disp_ref, f32[1,64,128]{2,1,0:T(8,128)S(1)} %get-tuple-element.5.dens_ref), custom_call_target="tpu_custom_call" | custom-call | tf_op jit(solution)/shard_map/pallas_call | solution.py:954
